TPU v7x, 32 devices: a whole 2x2x4 slice. The times are simulated.
32 devices in a mesh: dp: 8 (over z, y), inner: 4 (over x, core).
Axes of the slice: x: 2, y: 2, z: 4, core: 2. Of those that a mesh axis runs over, the one named last changes fastest.
Arguments:
- tokens: bfloat16 [32, 320, 1152], P(('dp', 'inner')), may hold values from -6 to 6
- time_vec: bfloat16 [32, 1152], P(('dp', 'inner')), may hold values from -6 to 6
- grid: int32 [32, 2], P(('dp', 'inner')), may hold values from 6 to 32, as said below
- cotangent: bfloat16 [32, 320, 1152], P(('dp', 'inner')), may hold values from -6 to 6
- gain_attn: float32 [1152], replicated, may hold values from 0.1 to 1.9
- gain_mlp: float32 [1152], replicated, may hold values from 0.1 to 1.9
- w_query: bfloat16 [1152, 1152], P('inner', 'dp'), may hold values from -0.1875 to 0.1875
- w_key: bfloat16 [1152, 1152], P('inner', 'dp'), may hold values from -0.1875 to 0.1875
- w_value: bfloat16 [1152, 1152], P('inner', 'dp'), may hold values from -0.1875 to 0.1875
- w_time_query: bfloat16 [1152, 1152], P('inner', 'dp'), may hold values from -0.1875 to 0.1875
- w_time_value: bfloat16 [1152, 1152], P('inner', 'dp'), may hold values from -0.1875 to 0.1875
- w_out: bfloat16 [1152, 1152], P('inner', 'dp'), may hold values from -1 to 1
- w_up: bfloat16 [1152, 4608], P('inner', 'dp'), may hold values from -0.1875 to 0.1875
- w_down: bfloat16 [4608, 1152], P('inner', 'dp'), may hold values from -0.09375 to 0.09375
- bias_rows: float32 [16, 63], replicated, may hold values from -3 to 3
- bias_cols: float32 [16, 63], replicated, may hold values from -3 to 3
Outputs:
- output: bfloat16 [32, 320, 1152], P(('dp', 'inner'))
- grad_tokens: bfloat16 [32, 320, 1152], P(('dp', 'inner'))
- grad_gain_attn: float32 [1152], replicated
- grad_gain_mlp: float32 [1152], replicated
- grad_w_query: float32 [1152, 1152], P('inner', 'dp')
- grad_w_key: float32 [1152, 1152], P('inner', 'dp')
- grad_w_value: float32 [1152, 1152], P('inner', 'dp')
- grad_w_time_query: float32 [1152, 1152], P('inner', 'dp')
- grad_w_time_value: float32 [1152, 1152], P('inner', 'dp')
- grad_w_out: float32 [1152, 1152], P('inner', 'dp')
- grad_w_up: float32 [1152, 4608], P('inner', 'dp')
- grad_w_down: float32 [4608, 1152], P('inner', 'dp')
- grad_bias_rows: float32 [16, 63], replicated
- grad_bias_cols: float32 [16, 63], replicated
Inputs may be any that keep to these rules, and one draw needn't show every extreme that they name: Each row holds an image's grid height and width, each at most 32, whose product lies between 192 and 320; some image has exactly 320 patches.
All inputs are finite; a program needn't handle non-finite values.
Results may differ from a plain program's by a relative error of at most 0.015.
Values may be sent and summed in bfloat16 or wider, within the bound.
A program may use at most 256 MiB of HBM per device.

v0:
```python
from functools import partial

import jax
import jax.numpy as jnp
from jax import lax
from jax.experimental import pallas as pl
from jax.experimental.pallas import tpu as pltpu
from jax.sharding import PartitionSpec as P

GS = 32
EPSILON = 1e-05
PRECISE = lax.Precision.HIGHEST
MESH = pl.DeviceIdType.MESH
AXES = ("dp", "inner")
SPOTS = 8


def place():
    dp, inner = lax.axis_index("dp"), lax.axis_index("inner")
    z, y = dp // 2, dp % 2
    return inner // 2, inner % 2, z + y * (7 - 2 * z)


def owner(x, core, spot):
    y = spot // 4
    z = spot + y * (7 - 2 * spot)
    return z * 2 + y, x * 2 + core


def ship(src, dst, send_sem, recv_sem, target):
    return pltpu.make_async_remote_copy(
        src_ref=src, dst_ref=dst, send_sem=send_sem, recv_sem=recv_sem, device_id=target, device_id_type=MESH
    )


def arrive(ref, sem):
    pltpu.make_async_copy(ref, ref, sem).wait()


def peers():
    x, core, spot = place()
    turn = 1 - 2 * core
    return (
        owner(x, core, (spot + turn + 8) % 8),
        owner(x, core, (spot - turn + 8) % 8),
        owner(1 - x, core, spot),
        owner(x, 1 - core, spot),
    )


def greet():
    barrier = pltpu.get_barrier_semaphore()
    for target in peers():
        pl.semaphore_signal(barrier, inc=1, device_id=target, device_id_type=MESH)
    pl.semaphore_wait(barrier, 4)


def every(count, body):
    def step(k, carry):
        body(k)
        return carry

    lax.fori_loop(0, count, step, 0)


class Gather:
    def __init__(self, home, pieces, early, ring_send, ring_recv, side_send, side_recv, pair_send, pair_recv):
        self.home, self.pieces, self.early = home, pieces, early
        self.ring, self.side, self.pair = (ring_send, ring_recv), (side_send, side_recv), (pair_send, pair_recv)
        self.x, self.core, self.spot = place()
        self.turn = 1 - 2 * self.core
        self.next, unused, self.across, self.partner = peers()

    @staticmethod
    def semaphores(pieces, early):
        dma = pltpu.SemaphoreType.DMA
        shapes = ((SPOTS - 1, pieces + early), (SPOTS, pieces), (SPOTS, 2 * pieces))
        return [dma(shape) for shape in shapes for twice in range(2)]

    def sent(self, pair, ref, slot, target):
        return ship(ref, ref, pair[0].at[slot], pair[1].at[slot], target)

    def who(self, step, plane):
        source = (self.spot - self.turn * step + 16) % 8
        return owner(self.x if plane == 0 else 1 - self.x, self.core, source)

    def step(self, step):
        for k in range(self.pieces):
            ref = self.home(k, self.who(step, 0))

            @pl.when(step > 0)
            def _():
                arrive(ref, self.ring[1].at[step - 1, k])

            @pl.when(step < SPOTS - 1)
            def _():
                self.sent(self.ring, ref, (step, k), self.next).start()

            if k >= self.early:
                self.sent(self.side, ref, (step, k), self.across).start()
            else:

                @pl.when(step == 0)
                def _():
                    self.sent(self.side, ref, (step, k), self.across).start()

            self.sent(self.pair, ref, (step, k), self.partner).start()
        for k in range(self.early):
            ref = self.home(k, self.who(step, 1))

            @pl.when(step == 0)
            def _():
                arrive(ref, self.side[1].at[step, k])

            @pl.when(step > 0)
            def _():
                arrive(ref, self.ring[1].at[step - 1, self.pieces + k])

            @pl.when(step < SPOTS - 1)
            def _():
                self.sent(self.ring, ref, (step, self.pieces + k), self.next).start()

            self.sent(self.pair, ref, (step, self.pieces + k), self.partner).start()

        @pl.when(step > 0)
        def _():
            self.crossed(step - 1)

    def crossed(self, step):
        for k in range(self.early, self.pieces):
            ref = self.home(k, self.who(step, 1))
            arrive(ref, self.side[1].at[step, k])
            self.sent(self.pair, ref, (step, self.pieces + k), self.partner).start()

    def finish(self):
        self.crossed(SPOTS - 1)

        def last(step):
            source = (self.spot + self.turn * step + 16) % 8
            for plane in range(2):
                who = owner(self.x if plane == 0 else 1 - self.x, 1 - self.core, source)
                for k in range(self.pieces):
                    arrive(self.home(k, who), self.pair[1].at[step, plane * self.pieces + k])
                    mine = self.home(k, self.who(step, plane))
                    self.sent(self.pair, mine, (step, plane * self.pieces + k), self.partner).wait_send()
            for k in range(self.pieces):
                ref = self.home(k, self.who(step, 0))

                @pl.when(step < SPOTS - 1)
                def _():
                    self.sent(self.ring, ref, (step, k), self.next).wait_send()

                if k >= self.early:
                    self.sent(self.side, ref, (step, k), self.across).wait_send()
                else:

                    @pl.when(step == 0)
                    def _():
                        self.sent(self.side, ref, (step, k), self.across).wait_send()

            for k in range(self.early):
                ref = self.home(k, self.who(step, 1))

                @pl.when(step < SPOTS - 1)
                def _():
                    self.sent(self.ring, ref, (step, self.pieces + k), self.next).wait_send()

        every(SPOTS, last)


def keep_own(refs, sem):
    copies = [pltpu.make_async_copy(src, dst, sem.at[k]) for k, (src, dst) in enumerate(refs)]
    for copy in copies:
        copy.start()
    for copy in copies:
        copy.wait()


def attention_gather_kernel(
    early, block, times, w_times, small_out, times_out, terms_out, time_buf, turned, own_sem, time_send, time_recv,
    term_send, term_recv, *sems,
):
    x, core, spot = place()
    me = owner(x, core, spot)
    here = me[0] * 4 + me[1]
    rows = block.shape[0]
    barrier = pltpu.get_barrier_semaphore()

    def other(k):
        place_of = (here + k) % 32
        return place_of, (place_of // 4, place_of % 4)

    def signal(k):
        pl.semaphore_signal(barrier, inc=1, device_id=other(k + 1)[1], device_id_type=MESH)

    every(31, signal)
    pl.semaphore_wait(barrier, 31)

    def home(k, who):
        lo, size = ((0, early), (early, rows - early))[k]
        return small_out.at[who[1], pl.ds(who[0] * rows + lo, size), :]

    def time_copy(k):
        there, target = other(k + 1)
        return ship(times.at[target[1]], time_buf.at[here], time_send.at[k], time_recv.at[k], target)

    def term_copy(k):
        there, target = other(k + 1)
        return ship(turned.at[there], terms_out.at[here], term_send.at[k], term_recv.at[k], target)

    every(31, lambda k: time_copy(k).start())
    time_buf[here] = times[me[1]]
    gather = Gather(home, 2, 1, *sems)
    keep_own([(block.at[pl.ds(0, early), :], home(0, me)), (block.at[pl.ds(early, rows - early), :], home(1, me))], own_sem)
    gather.step(0)
    every(31, lambda k: arrive(time_buf.at[(here + 31 - k) % 32], time_recv.at[k]))
    known = time_buf[...].reshape(32, time_buf.shape[2])
    times_out[...] = known
    terms = jnp.dot(known.astype(jnp.bfloat16), w_times[...], preferred_element_type=jnp.float32)
    turned[...] = terms.reshape(32, 1, terms.shape[1])
    every(31, lambda k: term_copy(k).start())
    terms_out[here] = turned[here]
    every(SPOTS - 1, lambda k: gather.step(k + 1))
    every(31, lambda k: arrive(terms_out.at[(here + 31 - k) % 32], term_recv.at[k]))

    def sent(k):
        time_copy(k).wait_send()
        term_copy(k).wait_send()

    every(31, sent)
    gather.finish()


def attention_gather(block, times, w_times):
    rows, width = block.shape
    early = rows * 4 // 9
    lanes = times.shape[2]
    dma = pltpu.SemaphoreType.DMA
    vmem = pl.BlockSpec(memory_space=pltpu.VMEM)
    return pl.pallas_call(
        partial(attention_gather_kernel, early),
        out_shape=(
            jax.ShapeDtypeStruct((4, SPOTS * rows, width), block.dtype),
            jax.ShapeDtypeStruct((32, lanes), jnp.float32),
            jax.ShapeDtypeStruct((32, 1, w_times.shape[1]), jnp.float32),
        ),
        in_specs=[vmem] * 3,
        out_specs=(pl.BlockSpec(memory_space=pl.ANY), vmem, vmem),
        scratch_shapes=[
            pltpu.VMEM((32, 1, lanes), jnp.float32),
            pltpu.VMEM((32, 1, w_times.shape[1]), jnp.float32),
            dma((2,)),
            dma((31,)),
            dma((31,)),
            dma((31,)),
            dma((31,)),
            *Gather.semaphores(2, 1),
        ],
        compiler_params=pltpu.CompilerParams(collective_id=0, has_side_effects=True),
        name="attention_gather",
    )(block, times, w_times)


def nt(a, b):
    return lax.dot_general(a, b, (((1,), (1,)), ((), ())), preferred_element_type=jnp.float32)


def nn(a, b):
    return lax.dot_general(a, b, (((1,), (0,)), ((), ())), preferred_element_type=jnp.float32)


def tn(a, b):
    return lax.dot_general(a, b, (((0,), (0,)), ((), ())), preferred_element_type=jnp.float32)


def attention_kernel(
    early, scale, block, small_in, normed, t_query, t_value, places, hots, mask, down_out, up_out, queries, keys, values,
    probs, attended, weights, own_sem, load_sem, *sems,
):
    x, core, spot = place()
    me = owner(x, core, spot)
    rows, width = block.shape[0] // 2, block.shape[1]
    size = rows // 2
    greet()
    loads = [pltpu.make_async_copy(small_in.at[k], weights.at[k], load_sem.at[k]) for k in range(3)]
    for copy in loads:
        copy.start()

    def home(k, who):
        j, i = who
        if k == 0:
            return down_out.at[pl.ds(j * rows, early), pl.ds(i * width, width)]
        if k == 1:
            return down_out.at[pl.ds(j * rows + early, rows - early), pl.ds(i * width, width)]
        return up_out.at[pl.ds((j * 4 + i) * rows, rows), :]

    gather = Gather(home, 3, 1, *sems)
    bounds = ((0, early), (early, rows - early), (rows, rows))
    keep_own([(block.at[pl.ds(*bounds[k]), :], home(k, me)) for k in range(3)], own_sem)

    def heads(p):
        known = normed[...]
        at = pl.ds(pl.multiple_of(p * rows, 16), rows)
        query = (nt(known, weights[0, at, :]) + t_query[p]).astype(jnp.bfloat16)
        key = nt(known, weights[1, at, :]).astype(jnp.bfloat16)
        value = (nt(known, weights[2, at, :]) + t_value[p]).astype(jnp.bfloat16)
        queries[p] = query
        keys[p] = key
        values[p] = value
        outs = []
        for t in range(2):
            part = slice(t * size, (t + 1) * size)
            scores = (nt(query[:, part], key[:, part]) + nt(places[2 * p + t], hots[...])) * scale
            scores = jnp.where(mask[...] > 0.0, scores, -1000000000.0)
            expo = jnp.exp(scores - jnp.max(scores, axis=-1, keepdims=True))
            low = (expo / jnp.sum(expo, axis=-1, keepdims=True)).astype(jnp.bfloat16)
            probs[2 * p + t] = low
            outs.append(nn(low, value[:, part]))
        attended[p] = jnp.concatenate(outs, axis=1).astype(jnp.bfloat16)

    def work(step):
        gather.step(step)

        @pl.when(step == 0)
        def _():
            for copy in loads:
                copy.wait()

        heads(step)

    every(SPOTS, work)
    gather.finish()


def attention_forward(block, small, normed, t_query, t_value, places, hots, mask, scale):
    rows, width = block.shape[0] // 2, block.shape[1]
    early = rows * 8 // 9
    slots = normed.shape[0]
    dma = pltpu.SemaphoreType.DMA
    vmem, far = pl.BlockSpec(memory_space=pltpu.VMEM), pl.BlockSpec(memory_space=pl.ANY)
    low = block.dtype
    pair = jax.ShapeDtypeStruct((SPOTS, slots, rows), low)
    return pl.pallas_call(
        partial(attention_kernel, early, scale),
        out_shape=(
            jax.ShapeDtypeStruct((SPOTS * rows, 4 * width), low),
            jax.ShapeDtypeStruct((32 * rows, width), low),
            pair,
            pair,
            pair,
            jax.ShapeDtypeStruct((2 * SPOTS, slots, slots), low),
            pair,
        ),
        in_specs=[vmem, far] + [vmem] * 6,
        out_specs=(far, far) + (vmem,) * 5,
        scratch_shapes=[
            pltpu.VMEM((3, SPOTS * rows, width), low),
            dma((3,)),
            dma((3,)),
            *Gather.semaphores(3, 1),
        ],
        compiler_params=pltpu.CompilerParams(collective_id=1, has_side_effects=True, vmem_limit_bytes=60 << 20),
        name="attention_forward",
    )(block, small, normed, t_query, t_value, places, hots, mask)


def pile(target, sources, size):
    tile = 16

    def body(k):
        total = None
        for ref, base in sources:
            piece = ref[pl.ds(pl.multiple_of(base + k * tile, 16), tile), :].astype(jnp.float32)
            total = piece if total is None else total + piece
        ref, base = target
        ref[pl.ds(pl.multiple_of(base + k * tile, 16), tile), :] = total.astype(ref.dtype)

    every(size // tile, body)


class Scatter:
    def __init__(
        self, home, parts, rows, early, result, pair_buf, ring_buf, side_buf, last_buf, own_buf, own_sem, ring_send,
        ring_recv, side_send, side_recv, last_send, last_recv, pair_send, pair_recv,
    ):
        self.home, self.parts, self.rows, self.early = home, parts, rows, early
        self.block = parts * rows
        self.result = result
        self.pair_buf, self.ring_buf, self.side_buf, self.last_buf, self.own_buf = (
            pair_buf, ring_buf, side_buf, last_buf, own_buf,
        )
        self.own_sem = own_sem
        self.ring, self.side, self.pair = (ring_send, ring_recv), (side_send, side_recv), (pair_send, pair_recv)
        self.last = (last_send, last_recv)
        self.x, self.core, self.spot = place()
        self.turn = 1 - 2 * self.core
        self.next, unused, self.across, self.partner = peers()

    @staticmethod
    def scratch(parts, rows, early, width, low):
        dma = pltpu.SemaphoreType.DMA
        block = parts * rows
        return [
            pltpu.VMEM((SPOTS, 2, block, width), low),
            pltpu.VMEM((SPOTS - 1, block + early, width), low),
            pltpu.VMEM((SPOTS, block - early, width), low),
            pltpu.VMEM((early, width), low),
            pltpu.VMEM((2, 2, block, width), low),
            dma((2, 2, parts)),
            dma((SPOTS - 1, 3)),
            dma((SPOTS - 1, 3)),
            dma((SPOTS,)),
            dma((SPOTS,)),
            dma((1,)),
            dma((1,)),
            dma((SPOTS, 2, parts)),
            dma((SPOTS, 2, parts)),
        ]

    def span(self, part):
        return pl.ds(part * self.rows, self.rows)

    def pair_copy(self, step, plane, part):
        goal = (self.spot + self.turn * (1 + step) + 16) % 8
        who = owner(self.x if plane == 0 else 1 - self.x, 1 - self.core, goal)
        return ship(
            self.home(part, who),
            self.pair_buf.at[step, plane, self.span(part), :],
            self.pair[0].at[step, plane, part],
            self.pair[1].at[step, plane, part],
            self.partner,
        )

    def begin(self):
        def give(step):
            for plane in (1, 0):
                for part in range(self.parts):
                    self.pair_copy(step, plane, part).start()

        every(SPOTS, give)
        self.fetch(0)

    def loads(self, step, plane):
        goal = (self.spot - self.turn * (1 + step) + 16) % 8
        who = owner(self.x if plane == 0 else 1 - self.x, self.core, goal)
        return [
            pltpu.make_async_copy(
                self.home(part, who),
                self.own_buf.at[step % 2, plane, self.span(part), :],
                self.own_sem.at[step % 2, plane, part],
            )
            for part in range(self.parts)
        ]

    def fetch(self, step):
        for plane in (1, 0):
            for copy in self.loads(step, plane):
                copy.start()

    def ready(self, step, plane):
        for copy in self.loads(step, plane):
            copy.wait()
        for part in range(self.parts):
            arrive(self.pair_buf.at[step, plane, self.span(part), :], self.pair[1].at[step, plane, part])

    def side_copy(self, step):
        src = self.pair_buf.at[step, 1, pl.ds(self.early, self.block - self.early), :]
        return ship(src, self.side_buf.at[step], self.side[0].at[step], self.side[1].at[step], self.across)

    def lane(self, n):
        return (
            (0, 0, 0, self.early),
            (0, self.early, self.early, self.block - self.early),
            (1, 0, self.block, self.early),
        )[n]

    def ring_copy(self, step, n):
        plane, lo, base, size = self.lane(n)
        return ship(
            self.pair_buf.at[step, plane, pl.ds(lo, size), :],
            self.ring_buf.at[step, pl.ds(base, size), :],
            self.ring[0].at[step, n],
            self.ring[1].at[step, n],
            self.next,
        )

    def sources(self, step, n, ring):
        plane, lo, base, size = self.lane(n)
        refs = [(self.own_buf.at[step % 2, plane], lo), (self.pair_buf.at[step, plane], lo)]
        if n == 1:
            refs.append((self.side_buf.at[step], 0))
        if ring:
            refs.append((self.ring_buf.at[step - 1], base))
        return refs

    def across_part(self, step):
        self.ready(step, 1)
        held = self.pair_buf.at[step, 1]
        mine = self.own_buf.at[step % 2, 1]
        pile((held, self.early), [(mine, self.early), (held, self.early)], self.block - self.early)
        self.side_copy(step).start()
        self.ready(step, 0)

    def step(self, step):
        self.across_part(step)
        self.fetch(step + 1)
        for n in range(3):
            plane, lo, base, size = self.lane(n)
            if n == 1:
                arrive(self.side_buf.at[step], self.side[1].at[step])

            @pl.when(step == 0)
            def _():
                pile((self.pair_buf.at[step, plane], lo), self.sources(step, n, False), size)

            @pl.when(step > 0)
            def _():
                arrive(self.ring_buf.at[step - 1, pl.ds(base, size), :], self.ring[1].at[step - 1, n])
                pile((self.pair_buf.at[step, plane], lo), self.sources(step, n, True), size)

            self.ring_copy(step, n).start()

    def finish(self):
        step = SPOTS - 1
        self.across_part(step)
        for n in (2, 1, 0):
            plane, lo, base, size = self.lane(n)
            arrive(self.ring_buf.at[step - 1, pl.ds(base, size), :], self.ring[1].at[step - 1, n])
            refs = self.sources(step, n, True)
            if n == 2:
                pile((self.pair_buf.at[step, 1], 0), refs, size)
                src = self.pair_buf.at[step, 1, pl.ds(0, size), :]
                over = ship(src, self.last_buf, self.last[0].at[0], self.last[1].at[0], self.across)
                over.start()
                continue
            if n == 1:
                arrive(self.side_buf.at[step], self.side[1].at[step])
            else:
                arrive(self.last_buf, self.last[1].at[0])
                refs.append((self.last_buf, 0))
            pile((self.result, lo), refs, size)
        over.wait_send()

        def sent(step):
            for plane in range(2):
                for part in range(self.parts):
                    self.pair_copy(step, plane, part).wait_send()
            self.side_copy(step).wait_send()

            @pl.when(step < SPOTS - 1)
            def _():
                for n in range(3):
                    self.ring_copy(step, n).wait_send()

        every(SPOTS, sent)


def backward_kernel(
    early, scale, down_in, up_in, small_in, normed, grad_attended, queries, keys, values, probs, hots, result, small_out,
    grad_normed, squares, sums, weights, load_sem, grads, grad_sem, *scratch,
):
    rows, width = result.shape[0] // 2, result.shape[1]
    size = rows // 2
    sides = hots.shape[1]
    greet()
    loads = [pltpu.make_async_copy(small_in.at[k], weights.at[k], load_sem.at[k]) for k in range(3)]
    for copy in loads:
        copy.start()

    def home(part, who):
        j, i = who
        if part == 0:
            return down_in.at[pl.ds(j * rows, rows), pl.ds(i * width, width)]
        return up_in.at[pl.ds((j * 4 + i) * rows, rows), :]

    scatter = Scatter(home, 2, rows, early, result, *scratch)
    scatter.begin()
    grad_normed[...] = jnp.zeros_like(grad_normed)

    def keep(p, k):
        return pltpu.make_async_copy(
            grads.at[p % 2, k], small_out.at[k, pl.ds(pl.multiple_of(p * rows, 16), rows), :], grad_sem.at[p % 2, k]
        )

    def heads(p):
        query, key, value, above = queries[p], keys[p], values[p], grad_attended[p]
        hot = hots[...]
        parts = ([], [], [])
        for t in range(2):
            part = slice(t * size, (t + 1) * size)
            low = probs[2 * p + t]
            wide = low.astype(jnp.float32)
            grad_probs = nt(above[:, part], value[:, part])
            inner = jnp.sum(wide * grad_probs, axis=-1, keepdims=True)
            grad_scores = (wide * (grad_probs - inner)).astype(jnp.bfloat16)
            parts[0].append(nn(grad_scores, key[:, part]) * scale)
            parts[1].append(tn(grad_scores, query[:, part]) * scale)
            parts[2].append(tn(low, above[:, part]))
            across = nn(grad_scores, hot)
            high = across.astype(jnp.bfloat16)
            rest = (across - high.astype(jnp.float32)).astype(jnp.bfloat16)
            squares[2 * p + t] = tn(hot, high) + tn(hot, rest)

        @pl.when(p >= 2)
        def _():
            for k in range(3):
                keep(p - 2, k).wait()

        known = normed[...]
        at = pl.ds(pl.multiple_of(p * rows, 16), rows)
        total = None
        for k in range(3):
            grad = jnp.concatenate(parts[k], axis=1).astype(jnp.bfloat16)
            sums[k, p] = jnp.sum(grad.astype(jnp.float32), axis=0, keepdims=True)
            grads[p % 2, k] = tn(grad, known).astype(jnp.bfloat16)
            keep(p, k).start()
            term = nn(grad, weights[k, at, :])
            total = term if total is None else total + term
        grad_normed[...] += total

    def work(step):
        @pl.when(step < SPOTS - 1)
        def _():
            scatter.step(step)

        @pl.when(step == 0)
        def _():
            for copy in loads:
                copy.wait()

        heads(step)

    every(SPOTS, work)
    for p in (SPOTS - 2, SPOTS - 1):
        for k in range(3):
            keep(p, k).wait()
    scatter.finish()


def attention_backward(down, up, small, normed, grad_attended, queries, keys, values, probs, hots, scale):
    rows, width = up.shape[0] // 32, up.shape[1]
    early = rows * 8 // 9
    slots = normed.shape[0]
    sides = hots.shape[1]
    low = up.dtype
    dma = pltpu.SemaphoreType.DMA
    vmem, far = pl.BlockSpec(memory_space=pltpu.VMEM), pl.BlockSpec(memory_space=pl.ANY)
    return pl.pallas_call(
        partial(backward_kernel, early, scale),
        out_shape=(
            jax.ShapeDtypeStruct((2 * rows, width), jnp.float32),
            jax.ShapeDtypeStruct((3, SPOTS * rows, width), low),
            jax.ShapeDtypeStruct((slots, width), jnp.float32),
            jax.ShapeDtypeStruct((2 * SPOTS, sides, sides), jnp.float32),
            jax.ShapeDtypeStruct((3, SPOTS, 1, rows), jnp.float32),
        ),
        in_specs=[far] * 3 + [vmem] * 7,
        out_specs=(vmem, far, vmem, vmem, vmem),
        scratch_shapes=[
            pltpu.VMEM((3, SPOTS * rows, width), low),
            dma((3,)),
            pltpu.VMEM((2, 3, rows, width), low),
            dma((2, 3)),
            *Scatter.scratch(2, rows, early, width, low),
        ],
        compiler_params=pltpu.CompilerParams(collective_id=2, has_side_effects=True, vmem_limit_bytes=63 << 20),
        name="attention_backward",
    )(down, up, small, normed, grad_attended, queries, keys, values, probs, hots)


def last_sums_kernel(early, small_in, out_in, extra_in, result, extra_out, own_sem, note_sems, scratch):
    x, core, spot = place()
    rows = result.shape[0]
    greet()

    def home(part, who):
        return small_in.at[who[1], pl.ds(who[0] * rows, rows), :]

    def note(k, who):
        return extra_out.at[who[0] * 4 + who[1]]

    scatter = Scatter(home, 1, rows, early, result, *scratch)
    scatter.begin()
    notes = Gather(note, 1, 1, *note_sems)
    keep_own([(extra_in, note(0, owner(x, core, spot)))], own_sem)

    def work(step):
        notes.step(step)

        @pl.when(step < SPOTS - 1)
        def _():
            scatter.step(step)

    every(SPOTS, work)
    scatter.finish()
    notes.finish()


def last_sums(small, extra):
    rows, width = small.shape[1] // SPOTS, small.shape[2]
    early = rows * 4 // 9
    low = small.dtype
    vmem, far = pl.BlockSpec(memory_space=pltpu.VMEM), pl.BlockSpec(memory_space=pl.ANY)

    def kernel(small_in, extra_in, result, extra_out, own_sem, *rest):
        last_sums_kernel(early, small_in, None, extra_in, result, extra_out, own_sem, rest[:6], rest[6:])

    return pl.pallas_call(
        kernel,
        out_shape=(
            jax.ShapeDtypeStruct((rows, width), jnp.float32),
            jax.ShapeDtypeStruct((32, *extra.shape), extra.dtype),
        ),
        in_specs=[far, vmem],
        out_specs=(vmem, vmem),
        scratch_shapes=[
            pltpu.SemaphoreType.DMA((1,)),
            *Gather.semaphores(1, 1),
            *Scatter.scratch(1, rows, early, width, low),
        ],
        compiler_params=pltpu.CompilerParams(collective_id=3, has_side_effects=True),
        name="last_sums",
    )(small, extra)


def layer_norm(matrix, gains):
    center = matrix - jnp.mean(matrix, axis=-1, keepdims=True)
    spread = jnp.mean(center * center, axis=-1, keepdims=True)
    return center * lax.rsqrt(spread + EPSILON) * gains


def slot_positions(grid, slots):
    heights = grid[:, 0]
    widths = grid[:, 1]
    length = heights * widths
    places = jnp.arange(slots, dtype=jnp.int32)
    usable = places[None, :] < length[:, None]
    clipped = jnp.minimum(places[None, :], length[:, None] - 1)
    return (usable, clipped // widths[:, None], clipped % widths[:, None])


def offset_table():
    shape = (GS, GS, 2 * GS - 1)
    source = lax.broadcasted_iota(jnp.int32, shape, 0)
    target = lax.broadcasted_iota(jnp.int32, shape, 1)
    offset = lax.broadcasted_iota(jnp.int32, shape, 2)
    return (source - target + (GS - 1) == offset).astype(jnp.float32)


def side_hot(places):
    sides = lax.broadcasted_iota(jnp.int32, (1, 1, GS), 2)
    return (places[:, :, None] == sides).astype(jnp.float32)


def position_bias(row_hot, col_hot, bias_rows, bias_cols, offset_hot):
    terms = []
    for hot_side, table in ((row_hot, bias_rows), (col_hot, bias_cols)):
        square = jnp.einsum("hd,rsd->hrs", table, offset_hot, precision=PRECISE)
        partial_rows = jnp.einsum("nir,hrs->nhis", hot_side, square, precision=PRECISE)
        terms.append(jnp.einsum("nhis,njs->nhij", partial_rows, hot_side, precision=PRECISE))
    return terms[0] + terms[1]


def bias_grads(grad_scores, row_hot, col_hot, offset_hot):
    results = []
    for hot_side in (row_hot, col_hot):
        partial_cols = jnp.einsum("nhij,njs->nhis", grad_scores, hot_side, precision=PRECISE)
        square = jnp.einsum("nir,nhis->hrs", hot_side, partial_cols, precision=PRECISE)
        results.append(jnp.einsum("hrs,rsd->hd", square, offset_hot, precision=PRECISE))
    return (results[0], results[1])


def masked_scores(queries, key_heads, position, usable):
    head_size = queries.shape[3]
    raw = jnp.einsum("nihe,njhe->nhij", queries, key_heads, preferred_element_type=jnp.float32)
    scores = raw * head_size ** (-0.5) + position
    return jnp.where(usable[:, None, None, :], scores, -1000000000.0)


def layer(tokens, grid, cotangent, gain_attn, gain_mlp, bias_rows, bias_cols, turned, time_query, time_value):
    images, slots, width = tokens.shape
    heads = bias_rows.shape[0]
    head_size = width // heads
    scale = head_size ** (-0.5)
    flat = images * slots
    gelu_tanh = partial(jax.nn.gelu, approximate=True)
    t_query, t_key, t_value, t_out, t_down, t_up = turned
    ahead = partial(jnp.einsum, "rd,ed->re", preferred_element_type=jnp.float32)
    back = partial(jnp.einsum, "re,ed->rd", preferred_element_type=jnp.float32)

    def outer(grads, values):
        return jnp.einsum("re,rd->ed", grads, values, preferred_element_type=jnp.float32).astype(jnp.bfloat16)

    inputs = tokens.astype(jnp.float32).reshape(flat, width)
    normed_attn = layer_norm(inputs, gain_attn).astype(jnp.bfloat16)
    shape = (images, slots, heads, head_size)
    queries = ahead(normed_attn, t_query).reshape(images, slots, width)
    queries = (queries + time_query[:, None, :]).astype(jnp.bfloat16).reshape(shape)
    key_heads = ahead(normed_attn, t_key).astype(jnp.bfloat16).reshape(shape)
    value_heads = ahead(normed_attn, t_value).reshape(images, slots, width)
    value_heads = (value_heads + time_value[:, None, :]).astype(jnp.bfloat16).reshape(shape)
    usable, row_place, col_place = slot_positions(grid, slots)
    offset_hot = offset_table()
    row_hot = side_hot(row_place)
    col_hot = side_hot(col_place)
    position = position_bias(row_hot, col_hot, bias_rows, bias_cols, offset_hot)
    scores = masked_scores(queries, key_heads, position, usable)
    maxima = jnp.max(scores, axis=-1, keepdims=True)
    expo = jnp.exp(scores - maxima)
    totals = jnp.sum(expo, axis=-1, keepdims=True)
    probs_low = (expo / totals).astype(jnp.bfloat16)
    attended = jnp.einsum("nhij,njhe->nihe", probs_low, value_heads, preferred_element_type=jnp.float32)
    attended = attended.astype(jnp.bfloat16).reshape(flat, width)
    mixed = inputs + ahead(attended, t_out)
    normed_mlp = layer_norm(mixed, gain_mlp).astype(jnp.bfloat16)
    up_proj = ahead(normed_mlp, t_up)
    hidden = gelu_tanh(up_proj).astype(jnp.bfloat16)
    keep_rows = usable.reshape(flat, 1)
    result = jnp.where(keep_rows, mixed + ahead(hidden, t_down), 0.0)
    output = result.astype(jnp.bfloat16).reshape(images, slots, width)
    upstream = jnp.where(keep_rows, cotangent.astype(jnp.float32).reshape(flat, width), 0.0)
    upstream_low = upstream.astype(jnp.bfloat16)
    grad_down = outer(upstream_low, hidden)
    grad_hidden = back(upstream_low, t_down)
    unused_gelu, gelu_back = jax.vjp(gelu_tanh, up_proj)
    grad_up_proj = gelu_back(grad_hidden)[0].astype(jnp.bfloat16)
    grad_up = outer(grad_up_proj, normed_mlp)
    grad_normed_mlp = back(grad_up_proj, t_up)
    unused_mlp, norm_mlp_back = jax.vjp(layer_norm, mixed, gain_mlp)
    grad_mixed_norm, grad_gain_mlp = norm_mlp_back(grad_normed_mlp)
    grad_mixed = upstream + grad_mixed_norm
    grad_mixed_low = grad_mixed.astype(jnp.bfloat16)
    grad_out = outer(grad_mixed_low, attended)
    grad_attended = back(grad_mixed_low, t_out).astype(jnp.bfloat16).reshape(shape)
    scores = masked_scores(queries, key_heads, position, usable)
    probs = jnp.exp(scores - maxima) / totals
    probs_low = probs.astype(jnp.bfloat16)
    grad_probs = jnp.einsum("nihe,njhe->nhij", grad_attended, value_heads, preferred_element_type=jnp.float32)
    inner_sum = jnp.sum(probs * grad_probs, axis=-1, keepdims=True)
    grad_scores = (probs * (grad_probs - inner_sum)).astype(jnp.bfloat16)
    grad_queries = jnp.einsum("nhij,njhe->nihe", grad_scores, key_heads, preferred_element_type=jnp.float32) * scale
    grad_queries = grad_queries.astype(jnp.bfloat16).reshape(images, slots, width)
    grad_keys = jnp.einsum("nhij,nihe->njhe", grad_scores, queries, preferred_element_type=jnp.float32) * scale
    grad_keys = grad_keys.astype(jnp.bfloat16).reshape(flat, width)
    grad_values = jnp.einsum("nhij,nihe->njhe", probs_low, grad_attended, preferred_element_type=jnp.float32)
    grad_values = grad_values.astype(jnp.bfloat16).reshape(images, slots, width)
    grad_rows_table, grad_cols_table = bias_grads(grad_scores.astype(jnp.float32), row_hot, col_hot, offset_hot)
    flat_queries = grad_queries.reshape(flat, width)
    flat_values = grad_values.reshape(flat, width)
    grad_query = outer(flat_queries, normed_attn)
    grad_key = outer(grad_keys, normed_attn)
    grad_value = outer(flat_values, normed_attn)
    slot_queries = jnp.sum(grad_queries.astype(jnp.float32), axis=1)
    slot_values = jnp.sum(grad_values.astype(jnp.float32), axis=1)
    grad_normed_attn = back(flat_queries, t_query) + back(grad_keys, t_key) + back(flat_values, t_value)
    unused_attn, norm_attn_back = jax.vjp(layer_norm, inputs, gain_attn)
    grad_inputs_norm, grad_gain_attn = norm_attn_back(grad_normed_attn)
    grad_tokens = (grad_mixed + grad_inputs_norm).astype(jnp.bfloat16).reshape(images, slots, width)
    return (
        output,
        grad_tokens,
        (grad_gain_attn, grad_gain_mlp, grad_rows_table, grad_cols_table, slot_queries, slot_values),
        (grad_query, grad_key, grad_value, grad_out, grad_down, grad_up),
    )


def time_terms(time_vec, w_time_query, w_time_value):
    all_times = lax.all_gather(time_vec, AXES, axis=0, tiled=True)
    rows = w_time_query.shape[0]
    mine = lax.dynamic_slice_in_dim(all_times, lax.axis_index("inner") * rows, rows, axis=1)
    both = jnp.concatenate([w_time_query, w_time_value], axis=1)
    return mine, jnp.dot(mine, both, preferred_element_type=jnp.float32)


def time_grads(mine, slot_sums, cols):
    column = lax.axis_index("dp") * cols
    picked = lax.dynamic_slice_in_dim(slot_sums, column, cols, axis=1)
    return jnp.einsum("nd,ne->de", mine.astype(jnp.float32), picked, precision=PRECISE)


def by_rings(
    tokens, time_vec, grid, cotangent, gain_attn, gain_mlp, w_query, w_key, w_value, w_time_query, w_time_value, w_out,
    w_up, w_down, bias_rows, bias_cols,
):
    images, slots, width = tokens.shape
    slab, rows = w_query.shape
    heads = bias_rows.shape[0]
    scale = (width // heads) ** (-0.5)
    gelu_tanh = partial(jax.nn.gelu, approximate=True)
    ahead = partial(jnp.einsum, "rd,ed->re", preferred_element_type=jnp.float32)
    back = partial(jnp.einsum, "re,ed->rd", preferred_element_type=jnp.float32)

    def outer(grads, values):
        return jnp.einsum("re,rd->ed", grads, values, preferred_element_type=jnp.float32).astype(jnp.bfloat16)

    small = jnp.stack([w_query.T, w_key.T, w_value.T, w_out.T])
    wide = w_up.T.reshape(4, rows, slab)
    swapped = lax.all_to_all(jnp.stack([small, wide], axis=1), "inner", 0, 0)
    joined = jnp.transpose(swapped, (1, 2, 0, 3)).reshape(2, rows, width)
    w_times = jnp.concatenate([w_time_query, w_time_value], axis=1)
    w_times = jnp.pad(w_times, ((0, -slab % 128), (0, -2 * rows % 128)))
    times = time_vec.astype(jnp.float32).reshape(4, 1, slab)
    times = jnp.pad(times, ((0, 0), (0, 0), (0, -slab % 128)))
    t_small, all_times, terms = attention_gather(joined[0], times, w_times)
    all_times = all_times[:, :slab]
    terms = terms.reshape(SPOTS, 4, -1)[:, :, : 2 * rows].sum(axis=1).reshape(SPOTS, 1, 2 * rows)

    inputs = tokens.astype(jnp.float32).reshape(slots, width)
    normed_attn = layer_norm(inputs, gain_attn).astype(jnp.bfloat16)
    usable, row_place, col_place = slot_positions(grid, slots)
    offset_hot = offset_table()
    hot = jnp.concatenate([side_hot(row_place)[0], side_hot(col_place)[0]], axis=1)
    squares = [
        jnp.einsum("hd,rsd->hrs", table, offset_hot, precision=PRECISE) for table in (bias_rows, bias_cols)
    ]
    places = jnp.concatenate(
        [
            jnp.einsum("ir,hrs->his", hot[:, GS * k : GS * (k + 1)], squares[k] / scale, precision=PRECISE)
            for k in range(2)
        ],
        axis=2,
    )
    high = lax.reduce_precision(places, 8, 7)
    places = jnp.concatenate([high, places - high], axis=2).astype(jnp.bfloat16)
    hot = hot.astype(jnp.bfloat16)
    hots = jnp.concatenate([hot, hot], axis=1)
    mask = usable.astype(jnp.float32)
    block = jnp.concatenate([w_down.T, joined[1]], axis=0)
    t_down, t_up, queries, keys, values, probs, attended = attention_forward(
        block, t_small, normed_attn, terms[:, :, :rows], terms[:, :, rows:], places, hots, mask, scale
    )
    attended = jnp.transpose(attended, (1, 0, 2)).reshape(slots, width)
    mixed = inputs + ahead(attended, t_small[3])
    normed_mlp = layer_norm(mixed, gain_mlp).astype(jnp.bfloat16)
    up_proj = ahead(normed_mlp, t_up)
    hidden = gelu_tanh(up_proj).astype(jnp.bfloat16)
    keep_rows = usable.reshape(slots, 1)
    result = jnp.where(keep_rows, mixed + ahead(hidden, t_down), 0.0)
    output = result.astype(jnp.bfloat16).reshape(images, slots, width)
    upstream = jnp.where(keep_rows, cotangent.astype(jnp.float32).reshape(slots, width), 0.0)
    upstream_low = upstream.astype(jnp.bfloat16)
    grad_down = outer(upstream_low, hidden)
    grad_hidden = back(upstream_low, t_down)
    unused_gelu, gelu_back = jax.vjp(gelu_tanh, up_proj)
    grad_up_proj = gelu_back(grad_hidden)[0].astype(jnp.bfloat16)
    grad_up = outer(grad_up_proj, normed_mlp)
    grad_normed_mlp = back(grad_up_proj, t_up)
    unused_mlp, norm_mlp_back = jax.vjp(layer_norm, mixed, gain_mlp)
    grad_mixed_norm, grad_gain_mlp = norm_mlp_back(grad_normed_mlp)
    grad_mixed = upstream + grad_mixed_norm
    grad_mixed_low = grad_mixed.astype(jnp.bfloat16)
    grad_out = outer(grad_mixed_low, attended)
    grad_attended = back(grad_mixed_low, t_small[3]).astype(jnp.bfloat16)
    grad_attended = jnp.transpose(grad_attended.reshape(slots, SPOTS, rows), (1, 0, 2))
    wide_block, small_grads, grad_normed_attn, table_squares, slot_sums = attention_backward(
        grad_down, grad_up, t_small, normed_attn, grad_attended, queries, keys, values, probs, hot, scale
    )
    unused_attn, norm_attn_back = jax.vjp(layer_norm, inputs, gain_attn)
    grad_inputs_norm, grad_gain_attn = norm_attn_back(grad_normed_attn)
    grad_tokens = (grad_mixed + grad_inputs_norm).astype(jnp.bfloat16).reshape(images, slots, width)
    tables = [
        jnp.einsum("hrs,rsd->hd", table_squares[:, cut, cut], offset_hot, precision=PRECISE)
        for cut in (slice(0, GS), slice(GS, 2 * GS))
    ]
    own = (grad_gain_attn, grad_gain_mlp, *tables, slot_sums[0], slot_sums[2])
    notes = jnp.stack([jnp.pad(value.reshape(-1), (0, width - value.size)) for value in own])
    notes = jnp.pad(notes, ((0, 2), (0, 0)))
    small_block, notes = last_sums(jnp.concatenate([small_grads, grad_out[None]], axis=0), notes)
    totals = notes[:, :4].sum(axis=0)
    entries = bias_rows.size
    table = bias_rows.shape
    joined = jnp.stack([small_block, wide_block[rows:]]).astype(jnp.bfloat16)
    parted = jnp.transpose(joined.reshape(2, rows, 4, slab), (2, 0, 1, 3))
    swapped = lax.all_to_all(parted, "inner", 0, 0).astype(jnp.float32)
    grad_small = jnp.transpose(swapped[:, 0], (0, 2, 1))
    grad_up = swapped[:, 1].reshape(4 * rows, slab).T
    grad_down = wide_block[:rows].T
    return (
        output,
        grad_tokens,
        totals[0],
        totals[1],
        grad_small[0],
        grad_small[1],
        grad_small[2],
        time_grads(all_times, notes[:, 4], rows),
        time_grads(all_times, notes[:, 5], rows),
        grad_small[3],
        grad_up,
        grad_down,
        totals[2, :entries].reshape(table),
        totals[3, :entries].reshape(table),
    )


def by_collectives(
    tokens, time_vec, grid, cotangent, gain_attn, gain_mlp, w_query, w_key, w_value, w_time_query, w_time_value, w_out,
    w_up, w_down, bias_rows, bias_cols,
):
    images, slots, width = tokens.shape
    cols = w_query.shape[1]
    mine_times, terms = time_terms(time_vec, w_time_query, w_time_value)
    terms = lax.psum(terms, "inner").reshape(-1, 2, cols)
    terms = lax.all_gather(terms, "dp", axis=2, tiled=True)
    here = (lax.axis_index("dp") * lax.psum(1, "inner") + lax.axis_index("inner")) * images
    terms = lax.dynamic_slice_in_dim(terms, here, images, axis=0)

    def whole(shard):
        part = lax.all_gather(shard, "inner", axis=0, tiled=True)
        return lax.all_gather(part, "dp", axis=1, tiled=True).T

    def shares(grad):
        part = lax.psum_scatter(grad.T, "inner", scatter_dimension=0, tiled=True)
        return lax.psum_scatter(part.astype(jnp.float32), "dp", scatter_dimension=1, tiled=True)

    turned = tuple(whole(shard) for shard in (w_query, w_key, w_value, w_out, w_down, w_up))
    output, grad_tokens, sums, grads = layer(
        tokens, grid, cotangent, gain_attn, gain_mlp, bias_rows, bias_cols, turned, terms[:, 0], terms[:, 1]
    )
    grad_query, grad_key, grad_value, grad_out, grad_down, grad_up = (shares(grad) for grad in grads)
    gain_a, gain_m, rows_table, cols_table = lax.psum(sums[:4], AXES)
    slot_queries, slot_values = (lax.all_gather(value, AXES, axis=0, tiled=True) for value in sums[4:])
    return (
        output, grad_tokens, gain_a, gain_m, grad_query, grad_key, grad_value,
        time_grads(mine_times, slot_queries, cols), time_grads(mine_times, slot_values, cols),
        grad_out, grad_up, grad_down, rows_table, cols_table,
    )


def solution(mesh):
    def local(*args):
        tokens, w_query = args[0], args[6]
        rings = dict(mesh.shape) == {"dp": SPOTS, "inner": 4} and tokens.shape[0] == 1
        rings = rings and w_query.shape[1] % 48 == 0 and tokens.shape[2] % 128 == 0
        return (by_rings if rings else by_collectives)(*args)

    data, weight = P(AXES, None, None), P("inner", "dp")
    return jax.shard_map(
        local,
        mesh=mesh,
        in_specs=(data, P(AXES, None), P(AXES, None), data, P(), P(), *(weight,) * 8, P(), P()),
        out_specs=(data, data, P(), P(), *(weight,) * 8, P(), P()),
        check_vma=False,
    )
```

profile of v0, /device:TPU:0, one launch (start us, length us, event | category | flops | bytes accessed | tf_op | source)
XLA Modules:
  0.0 469.0 jit_solution(10789774802804942158)
XLA Ops:
  4.3 4.4 all-to-all-start
  16.7 2.7 convolution_bitcast_fusion
  20.7 2.8 convolution_bitcast_fusion.1
  25.2 3.3 reduce-precision_convert_fusion
  33.3 57.9 %attention_gather.1 = (bf16[4,1152,1152]{2,1,0:T(8,128)(2,1)}, f32[32,384]{1,0:T(8,128)}, f32[32,1,384]{2,1,0:T(1,128)}) custom-call(bf16[144,1152]{1,0:T(8,128)(2,1)} %squeeze.38.block, f32[4,1,384]{2,1,0:T(1,128)} %pad_convert_fusion.times, bf16[384,384]{1,0:T(8,128)(2,1)} %fusion.43.w_times), custom_call_target="tpu_custom_call" | custom-call | tf_op jit(solution)/shard_map/attention_gather/pallas_call | solution.py:240
  93.8 92.0 %attention_forward.1 = (bf16[1152,4608]{1,0:T(8,128)(2,1)}, bf16[4608,1152]{1,0:T(8,128)(2,1)}, bf16[8,320,144]{2,1,0:T(8,128)(2,1)}, bf16[8,320,144]{2,1,0:T(8,...) custom-call(bf16[288,1152]{1,0:T(8,128)(2,1)} %pad_maximum_fusion.4.block, ...), custom_call_target="tpu_custom_call" | custom-call | tf_op jit(solution)/shard_map/attention_forward/pallas_call | solution.py:343
  185.7 2.0 copy.75
  187.7 3.3 fusion.82
  191.7 6.9 %fusion.75 = f32[320,4608]{1,0:T(8,128)S(1)} fusion(bf16[4608,1152]{1,0:T(8,128)(2,1)} %get-tuple-element.34, f32[320,1152]{1,0:T(8,128)S(1)} %get-tuple-element.105, f32[1152]{0:T(1024)S(1)} %copy-done.18, f32[320]{0:T(512)S(1)} %fusion.67, f32[320]{0:T(512)S(1)} %broadcast_multiply_fusion), kind=kOutput, calls=%fused_computation.145 | convolution fusion | flops 3398860800 | bytes 17996800 | tf_op jit(solution)/shard_map/rd,ed->re/dot_general | solution.py:935
  198.6 9.5 %fusion.13 = bf16[1,320,1152]{2,1,0:T(8,128)(2,1)} fusion(f32[320,1152]{1,0:T(8,128)S(1)} %get-tuple-element.105, bf16[1152,4608]{1,0:T(8,128)(2,1)} %get-tuple-element.35, pred[320]{0:T(512)(128)(4,1)S(1)} %iota_compare_fusion.9, f32[320,4608]{1,0:T(8,128)S(1)} %fusion.75), kind=kOutput, calls=%fused_computation.26 | convolution fusion | flops 3411763200 | bytes 18727232 | tf_op jit(solution)/shard_map/rd,ed->re/dot_general | solution.py:938
  208.1 9.2 %fusion.7 = bf16[320,4608]{1,0:T(8,128)(2,1)S(1)} fusion(f32[320,4608]{1,0:T(8,128)S(1)} %fusion.75, bf16[1152,4608]{1,0:T(8,128)(2,1)} %get-tuple-element.35, bf16[1,320,1152]{2,1,0:T(8,128)(2,1)S(1)} %copy-done.6, pred[320]{0:T(512)(128)(4,1)S(1)} %iota_compare_fusion.9), kind=kOutput, calls=%fused_computation.13 | convolution fusion | flops 3427983360 | bytes 20201792 | tf_op jit(solution)/shard_map/re,ed->rd/dot_general | solution.py:943
  217.4 9.2 %convolution_convert_fusion.1.down_in = bf16[1152,4608]{1,0:T(8,128)(2,1)} fusion(bf16[1,320,1152]{2,1,0:T(8,128)(2,1)S(1)} %copy-done.6, pred[320]{0:T(512)(128)(4,1)S(1)} %iota_compare_fusion.9, f32[320,4608]{1,0:T(8,128)S(1)} %fusion.75), kind=kOutput, calls=%fused_computation.1 | convolution fusion | flops 3417071616 | bytes 17252672 | tf_op jit(solution)/shard_map/re,rd->ed/dot_general | solution.py:894
  226.6 8.2 %multiply_reduce_fusion = (f32[1152]{0:T(1024)S(1)}, f32[320]{0:T(512)S(1)}, f32[320,1152]{1,0:T(8,128)S(1)}) fusion(f32[320,1152]{1,0:T(8,128)S(1)} %get-tuple-element.105, f32[320]{0:T(512)S(1)} %fusion.67, f32[320]{0:T(512)S(1)} %broadcast_multiply_fusion, f32[1152]{0:T(1024)S(1)} %copy-done.18, bf16[320,4608]{1,0:T(8,128)(2,1)S(1)} %fusion.7, ...), kind=kOutput, calls=%fused_computation.49 | convolution fusion | flops 3399965440 | bytes 16528128 | tf_op jit(solution)/shard_map/re,ed->rd/dot_general | solution.py:947
  234.7 9.1 %convolution_convert_fusion.up_in = bf16[4608,1152]{1,0:T(8,128)(2,1)} fusion(bf16[320,4608]{1,0:T(8,128)(2,1)S(1)} %fusion.7, f32[320,1152]{1,0:T(8,128)S(1)} %get-tuple-element.105, f32[1152]{0:T(1024)S(1)} %copy-done.18, f32[320]{0:T(512)S(1)} %fusion.67, f32[320]{0:T(512)S(1)} %broadcast_multiply_fusion), kind=kOutput, calls=%fused_computation | convolution fusion | flops 3404169216 | bytes 15047680 | tf_op jit(solution)/shard_map/re,rd->ed/dot_general | solution.py:894
  245.5 3.0 convolution_convert_fusion.3
  248.5 3.2 fusion
  254.0 111.2 %attention_backward.1 = (f32[288,1152]{1,0:T(8,128)}, bf16[3,1152,1152]{2,1,0:T(8,128)(2,1)}, f32[320,1152]{1,0:T(8,128)}, f32[16,64,64]{2,1,0:T(8,128)}, f32[3,8,1,144]{3,2,1,0:T(1,128)}) custom-call(bf16[1152,4608]{1,0:T(8,128)(2,1)} %convolution_convert_fusion.1.down_in, bf16[4608,1152]{1,0:T(8,128)(2,1)} %convolution_convert_fusion.up_in, ...), custom_call_target="tpu_custom_call" | custom-call | tf_op jit(solution)/shard_map/attention_backward/pallas_call | solution.py:648
  365.3 1.9 fusion.26
  370.7 10.0 %pad_maximum_fusion.small_in = bf16[4,1152,1152]{2,1,0:T(8,128)(2,1)} fusion(bf16[1,1152,1152]{2,1,0:T(8,128)(2,1)} %fusion, bf16[3,1152,1152]{2,1,0:T(8,128)(2,1)} %get-tuple-element.41), kind=kLoop, calls=%fused_computation.2 | loop fusion | flops 5308416 | bytes 21233664 | tf_op jit(solution)/shard_map/concatenate | solution.py:968
  380.7 59.1 %last_sums.1 = (f32[144,1152]{1,0:T(8,128)}, f32[32,8,1152]{2,1,0:T(8,128)}) custom-call(bf16[4,1152,1152]{2,1,0:T(8,128)(2,1)} %pad_maximum_fusion.small_in, f32[8,1152]{1,0:T(8,128)} %pad.26.extra_in), custom_call_target="tpu_custom_call" | custom-call | tf_op jit(solution)/shard_map/last_sums/pallas_call | solution.py:708
  441.2 1.9 fusion.77
  443.8 3.0 fusion.32
  450.1 3.6 all-to-all-start.1
  458.4 8.0 %all-to-all-done.1 = bf16[4,2,144,288]{3,2,1,0:T(8,128)(2,1)S(1)} async-done(((bf16[4,2,144,288]{3,2,1,0:T(8,128)(2,1)}), bf16[4,2,144,288]{3,2,1,0:T(8,128)(2,1)S(1)}, u32[]{:S(2)}, u32[]{:S(2)}) %all-to-all-start.1) | async-done | bytes 663584 | tf_op jit(solution)/shard_map/all_to_all | solution.py:974
  (132 shorter events, 39.0 us)
Async XLA Ops:
  0.6 12.7 %copy-start = (f32[16,63]{1,0:T(8,128)S(1)}, f32[16,63]{1,0:T(8,128)}, u32[]{:S(2)}) copy-start(f32[16,63]{1,0:T(8,128)} %param.31) | copy-start | bytes 12100
  3.2 5.4 %copy-start.20 = (s32[1,2]{1,0:T(1,128)S(1)}, s32[1,2]{1,0:T(1,128)}, u32[]{:S(2)}) copy-start(s32[1,2]{1,0:T(1,128)} %param.18) | copy-start | bytes 28
  3.3 8.5 %copy-start.19 = (bf16[1,1152]{1,0:T(2,128)(2,1)S(1)}, bf16[1,1152]{1,0:T(2,128)(2,1)}, u32[]{:S(2)}) copy-start(bf16[1,1152]{1,0:T(2,128)(2,1)} %param.17) | copy-start | bytes 6916
  3.3 9.3 %copy-start.15 = (bf16[288,144]{0,1:T(8,128)(2,1)S(1)}, bf16[288,144]{0,1:T(8,128)(2,1)}, u32[]{:S(2)}) copy-start(bf16[288,144]{0,1:T(8,128)(2,1)} %param.26) | copy-start | bytes 248836
  4.3 8.3 %copy-start.16 = (bf16[288,144]{0,1:T(8,128)(2,1)S(1)}, bf16[288,144]{0,1:T(8,128)(2,1)}, u32[]{:S(2)}) copy-start(bf16[288,144]{0,1:T(8,128)(2,1)} %param.25) | copy-start | bytes 248836
  4.3 8.5 %copy-start.2 = (bf16[1,320,1152]{2,1,0:T(8,128)(2,1)S(1)}, bf16[1,320,1152]{2,1,0:T(8,128)(2,1)}, u32[]{:S(2)}) copy-start(bf16[1,320,1152]{2,1,0:T(8,128)(2,1)} %param.16) | copy-start | bytes 2211844
  4.3 27.2 %all-to-all-start = ((bf16[4,2,144,288]{3,2,1,0:T(8,128)(2,1)}), bf16[4,2,144,288]{3,2,1,0:T(8,128)(2,1)S(1)}, u32[]{:S(2)}, u32[]{:S(2)}) async-start(bf16[4,2,144,288]{3,2,1,0:T(8,128)(2,1)} %copy.63), calls=%async_computation | async-start | bytes 1769472 | tf_op jit(solution)/shard_map/all_to_all | solution.py:898
  15.8 3.6 copy-start.21
  23.6 4.9 %copy-start.9 = (bf16[320,64]{1,0:T(8,128)(2,1)}, bf16[320,64]{1,0:T(8,128)(2,1)S(1)}, u32[]{:S(2)}) copy-start(bf16[320,64]{1,0:T(8,128)(2,1)S(1)} %convert_convert_fusion.hots) | copy-start | bytes 122884
  28.5 1.8 copy-start.14
  32.1 60.8 %copy-start.12 = (bf16[1152,144]{0,1:T(8,128)(2,1)S(1)}, bf16[1152,144]{0,1:T(8,128)(2,1)}, u32[]{:S(2)}) copy-start(bf16[1152,144]{0,1:T(8,128)(2,1)} %param.29) | copy-start | bytes 995332
  191.0 0.7 copy-start.18
  198.6 9.5 %copy-start.6 = (bf16[1,320,1152]{2,1,0:T(8,128)(2,1)S(1)}, bf16[1,320,1152]{2,1,0:T(8,128)(2,1)}, u32[]{:S(2)}) copy-start(bf16[1,320,1152]{2,1,0:T(8,128)(2,1)} %param.19) | copy-start | bytes 2211844
  244.4 1.1 copy-start.3
  365.3 1.9 copy-start.5
  367.2 1.0 copy-start.11
  368.0 1.8 copy-start.17
  380.7 63.1 %copy-start.4 = (f32[320,1152]{1,0:T(8,128)S(1)}, f32[320,1152]{1,0:T(8,128)}, u32[]{:S(2)}) copy-start(f32[320,1152]{1,0:T(8,128)} %copy-done.3) | copy-start | bytes 4423684
  439.8 4.0 copy-start.7
  446.8 1.7 copy-start.10
  449.0 5.0 %copy-start.13 = (f32[32,384]{1,0:T(8,128)S(1)}, f32[32,384]{1,0:T(8,128)}, u32[]{:S(2)}) copy-start(f32[32,384]{1,0:T(8,128)} %get-tuple-element.47) | copy-start | bytes 147460
  450.1 7.4 %copy-start.8 = (f32[288,1152]{1,0:T(8,128)S(1)}, f32[288,1152]{1,0:T(8,128)}, u32[]{:S(2)}) copy-start(f32[288,1152]{1,0:T(8,128)} %get-tuple-element.46) | copy-start | bytes 3981316
  450.1 16.3 %all-to-all-start.1 = ((bf16[4,2,144,288]{3,2,1,0:T(8,128)(2,1)}), bf16[4,2,144,288]{3,2,1,0:T(8,128)(2,1)S(1)}, u32[]{:S(2)}, u32[]{:S(2)}) async-start(bf16[4,2,144,288]{3,2,1,0:T(8,128)(2,1)} %maximum_bitcast_fusion), calls=%async_computation.1 | async-start | bytes 1769472 | tf_op jit(solution)/shard_map/all_to_all | solution.py:974
  466.6 2.2 copy-start.1
where the time goes:
time: 478 us; the launch traced here: 469 us
  Pallas kernels  320 us (67%)
  matrix products  72.5 us (15%)
  other arithmetic  33.3 us (7%)
  local copies, waits for them, and re-layouts  22.2 us (5%)
  starting transfers between devices  8 us (2%)
  waiting for transfers between devices  7.97 us (2%)
    pallas_call x1, Pallas kernels, attention_backward(): pl.pallas_call(partial(backward_kernel, early, scale), out_shape=(jax.Sha...  111 us
    pallas_call x1, Pallas kernels, attention_forward(): pl.pallas_call(partial(attention_kernel, early, scale), out_shape=(jax.Sh...  92 us
    pallas_call x1, Pallas kernels, last_sums(): pl.pallas_call(kernel, out_shape=(jax.ShapeDtypeStruct((rows, width), jnp...  59.1 us
    pallas_call x1, Pallas kernels, attention_gather(): pl.pallas_call(partial(attention_gather_kernel, early), out_shape=(jax.Sh...  57.9 us
    dot_general x3, matrix products, outer(): jnp.einsum('re,rd->ed', grads, values, preferred_element_type=jnp.float32)  21.4 us
    concatenate x1, other arithmetic, by_rings(): jnp.concatenate([small_grads, grad_out[None]], axis=0)  9.99 us
  transfers between devices with their start and end apart: 2, of which 1 were waited for; matrix products, arithmetic and copies ran while one was open for 5% of the time, Pallas kernels for 0%

commit v1 on v0

--- a/solution.py
+++ b/solution.py
@@ -64,12 +64,13 @@
 
 
 class Gather:
-    def __init__(self, home, pieces, early, ring_send, ring_recv, side_send, side_recv, pair_send, pair_recv):
-        self.home, self.pieces, self.early = home, pieces, early
+    def __init__(self, own, home, pieces, early, ring_send, ring_recv, side_send, side_recv, pair_send, pair_recv):
+        self.own, self.home, self.pieces, self.early = own, home, pieces, early
         self.ring, self.side, self.pair = (ring_send, ring_recv), (side_send, side_recv), (pair_send, pair_recv)
         self.x, self.core, self.spot = place()
         self.turn = 1 - 2 * self.core
         self.next, unused, self.across, self.partner = peers()
+        self.order = [*range(early, pieces), *range(early)]
 
     @staticmethod
     def semaphores(pieces, early):
@@ -77,34 +78,46 @@
         shapes = ((SPOTS - 1, pieces + early), (SPOTS, pieces), (SPOTS, 2 * pieces))
         return [dma(shape) for shape in shapes for twice in range(2)]
 
-    def sent(self, pair, ref, slot, target):
-        return ship(ref, ref, pair[0].at[slot], pair[1].at[slot], target)
+    def sent(self, pair, ref, slot, target, src=None):
+        return ship(ref if src is None else src, ref, pair[0].at[slot], pair[1].at[slot], target)
 
     def who(self, step, plane):
         source = (self.spot - self.turn * step + 16) % 8
         return owner(self.x if plane == 0 else 1 - self.x, self.core, source)
 
+    def start(self, own_sem):
+        me = self.who(0, 0)
+        for k in range(self.early):
+            self.sent(self.side, self.home(k, me), (0, k), self.across, self.own(k)).start()
+        for k in self.order:
+            ref, src = self.home(k, me), self.own(k)
+            self.sent(self.ring, ref, (0, k), self.next, src).start()
+            if k >= self.early:
+                self.sent(self.side, ref, (0, k), self.across, src).start()
+        for k in self.order:
+            ref, src = self.home(k, me), self.own(k)
+            self.sent(self.pair, ref, (0, k), self.partner, src).start()
+            pltpu.make_async_copy(src, ref, own_sem.at[k]).start()
+
+    def kept(self, own_sem):
+        for k in range(self.pieces):
+            pltpu.make_async_copy(self.own(k), self.home(k, self.who(0, 0)), own_sem.at[k]).wait()
+
     def step(self, step):
-        for k in range(self.pieces):
-            ref = self.home(k, self.who(step, 0))
-
-            @pl.when(step > 0)
-            def _():
+        @pl.when(step > 0)
+        def _():
+            for k in self.order:
+                ref = self.home(k, self.who(step, 0))
                 arrive(ref, self.ring[1].at[step - 1, k])
 
-            @pl.when(step < SPOTS - 1)
-            def _():
-                self.sent(self.ring, ref, (step, k), self.next).start()
-
-            if k >= self.early:
-                self.sent(self.side, ref, (step, k), self.across).start()
-            else:
-
-                @pl.when(step == 0)
+                @pl.when(step < SPOTS - 1)
                 def _():
+                    self.sent(self.ring, ref, (step, k), self.next).start()
+
+                if k >= self.early:
                     self.sent(self.side, ref, (step, k), self.across).start()
-
-            self.sent(self.pair, ref, (step, k), self.partner).start()
+                self.sent(self.pair, ref, (step, k), self.partner).start()
+
         for k in range(self.early):
             ref = self.home(k, self.who(step, 1))
 
@@ -132,15 +145,20 @@
             arrive(ref, self.side[1].at[step, k])
             self.sent(self.pair, ref, (step, self.pieces + k), self.partner).start()
 
-    def finish(self):
-        self.crossed(SPOTS - 1)
-
+    def all_here(self):
         def last(step):
             source = (self.spot + self.turn * step + 16) % 8
             for plane in range(2):
                 who = owner(self.x if plane == 0 else 1 - self.x, 1 - self.core, source)
                 for k in range(self.pieces):
                     arrive(self.home(k, who), self.pair[1].at[step, plane * self.pieces + k])
+
+        every(SPOTS, last)
+
+    def drain(self):
+        def last(step):
+            for plane in range(2):
+                for k in range(self.pieces):
                     mine = self.home(k, self.who(step, plane))
                     self.sent(self.pair, mine, (step, plane * self.pieces + k), self.partner).wait_send()
             for k in range(self.pieces):
@@ -168,37 +186,39 @@
         every(SPOTS, last)
 
 
-def keep_own(refs, sem):
-    copies = [pltpu.make_async_copy(src, dst, sem.at[k]) for k, (src, dst) in enumerate(refs)]
-    for copy in copies:
-        copy.start()
-    for copy in copies:
-        copy.wait()
-
-
-def attention_gather_kernel(
-    early, block, times, w_times, small_out, times_out, terms_out, time_buf, turned, own_sem, time_send, time_recv,
-    term_send, term_recv, *sems,
+def nt(a, b):
+    return lax.dot_general(a, b, (((1,), (1,)), ((), ())), preferred_element_type=jnp.float32)
+
+
+def nn(a, b):
+    return lax.dot_general(a, b, (((1,), (0,)), ((), ())), preferred_element_type=jnp.float32)
+
+
+def tn(a, b):
+    return lax.dot_general(a, b, (((0,), (0,)), ((), ())), preferred_element_type=jnp.float32)
+
+
+def forward_kernel(
+    small_early, early, scale, small_block, block, times, w_times, normed, squares, hots, mask, down_out, up_out,
+    turned_out, times_out, queries, keys, values, probs, attended, shards, turned, time_buf, term_buf, terms, own_sem,
+    turn_sem, time_send, time_recv, term_send, term_recv, *sems,
 ):
     x, core, spot = place()
     me = owner(x, core, spot)
     here = me[0] * 4 + me[1]
-    rows = block.shape[0]
+    rows, width = small_block.shape
+    size, slab = rows // 2, width // 4
     barrier = pltpu.get_barrier_semaphore()
 
     def other(k):
-        place_of = (here + k) % 32
-        return place_of, (place_of // 4, place_of % 4)
+        there = (here + k) % 32
+        return there, (there // 4, there % 4)
 
     def signal(k):
         pl.semaphore_signal(barrier, inc=1, device_id=other(k + 1)[1], device_id_type=MESH)
 
     every(31, signal)
     pl.semaphore_wait(barrier, 31)
-
-    def home(k, who):
-        lo, size = ((0, early), (early, rows - early))[k]
-        return small_out.at[who[1], pl.ds(who[0] * rows + lo, size), :]
 
     def time_copy(k):
         there, target = other(k + 1)
@@ -206,85 +226,26 @@
 
     def term_copy(k):
         there, target = other(k + 1)
-        return ship(turned.at[there], terms_out.at[here], term_send.at[k], term_recv.at[k], target)
+        return ship(term_buf.at[there], terms.at[here], term_send.at[k], term_recv.at[k], target)
+
+    def project():
+        every(31, lambda k: arrive(time_buf.at[(here + 31 - k) % 32], time_recv.at[k]))
+        known = time_buf[...].reshape(32, time_buf.shape[2])
+        times_out[...] = known
+        found = jnp.dot(known.astype(jnp.bfloat16), w_times[...], preferred_element_type=jnp.float32)
+        term_buf[...] = found.reshape(32, 1, found.shape[1])
+        every(31, lambda k: term_copy(k).start())
+        terms[here] = term_buf[here]
 
     every(31, lambda k: time_copy(k).start())
     time_buf[here] = times[me[1]]
-    gather = Gather(home, 2, 1, *sems)
-    keep_own([(block.at[pl.ds(0, early), :], home(0, me)), (block.at[pl.ds(early, rows - early), :], home(1, me))], own_sem)
-    gather.step(0)
-    every(31, lambda k: arrive(time_buf.at[(here + 31 - k) % 32], time_recv.at[k]))
-    known = time_buf[...].reshape(32, time_buf.shape[2])
-    times_out[...] = known
-    terms = jnp.dot(known.astype(jnp.bfloat16), w_times[...], preferred_element_type=jnp.float32)
-    turned[...] = terms.reshape(32, 1, terms.shape[1])
-    every(31, lambda k: term_copy(k).start())
-    terms_out[here] = turned[here]
-    every(SPOTS - 1, lambda k: gather.step(k + 1))
-    every(31, lambda k: arrive(terms_out.at[(here + 31 - k) % 32], term_recv.at[k]))
-
-    def sent(k):
-        time_copy(k).wait_send()
-        term_copy(k).wait_send()
-
-    every(31, sent)
-    gather.finish()
-
-
-def attention_gather(block, times, w_times):
-    rows, width = block.shape
-    early = rows * 4 // 9
-    lanes = times.shape[2]
-    dma = pltpu.SemaphoreType.DMA
-    vmem = pl.BlockSpec(memory_space=pltpu.VMEM)
-    return pl.pallas_call(
-        partial(attention_gather_kernel, early),
-        out_shape=(
-            jax.ShapeDtypeStruct((4, SPOTS * rows, width), block.dtype),
-            jax.ShapeDtypeStruct((32, lanes), jnp.float32),
-            jax.ShapeDtypeStruct((32, 1, w_times.shape[1]), jnp.float32),
-        ),
-        in_specs=[vmem] * 3,
-        out_specs=(pl.BlockSpec(memory_space=pl.ANY), vmem, vmem),
-        scratch_shapes=[
-            pltpu.VMEM((32, 1, lanes), jnp.float32),
-            pltpu.VMEM((32, 1, w_times.shape[1]), jnp.float32),
-            dma((2,)),
-            dma((31,)),
-            dma((31,)),
-            dma((31,)),
-            dma((31,)),
-            *Gather.semaphores(2, 1),
-        ],
-        compiler_params=pltpu.CompilerParams(collective_id=0, has_side_effects=True),
-        name="attention_gather",
-    )(block, times, w_times)
-
-
-def nt(a, b):
-    return lax.dot_general(a, b, (((1,), (1,)), ((), ())), preferred_element_type=jnp.float32)
-
-
-def nn(a, b):
-    return lax.dot_general(a, b, (((1,), (0,)), ((), ())), preferred_element_type=jnp.float32)
-
-
-def tn(a, b):
-    return lax.dot_general(a, b, (((0,), (0,)), ((), ())), preferred_element_type=jnp.float32)
-
-
-def attention_kernel(
-    early, scale, block, small_in, normed, t_query, t_value, places, hots, mask, down_out, up_out, queries, keys, values,
-    probs, attended, weights, own_sem, load_sem, *sems,
-):
-    x, core, spot = place()
-    me = owner(x, core, spot)
-    rows, width = block.shape[0] // 2, block.shape[1]
-    size = rows // 2
-    greet()
-    loads = [pltpu.make_async_copy(small_in.at[k], weights.at[k], load_sem.at[k]) for k in range(3)]
-    for copy in loads:
-        copy.start()
+
+    small_bounds = ((0, small_early), (small_early, rows - small_early))
+    bounds = ((0, early), (early, rows - early), (rows, rows))
+
+    def small_home(k, who):
+        lo, span = small_bounds[k]
+        return shards.at[who[1], pl.ds(who[0] * rows + lo, span), :]
 
     def home(k, who):
         j, i = who
@@ -294,23 +255,43 @@
             return down_out.at[pl.ds(j * rows + early, rows - early), pl.ds(i * width, width)]
         return up_out.at[pl.ds((j * 4 + i) * rows, rows), :]
 
-    gather = Gather(home, 3, 1, *sems)
-    bounds = ((0, early), (early, rows - early), (rows, rows))
-    keep_own([(block.at[pl.ds(*bounds[k]), :], home(k, me)) for k in range(3)], own_sem)
+    small = Gather(lambda k: small_block.at[pl.ds(*small_bounds[k]), :], small_home, 2, 1, *sems[:6])
+    large = Gather(lambda k: block.at[pl.ds(*bounds[k]), :], home, 3, 1, *sems[6:])
+
+    def keep(p, k):
+        at = pl.ds(pl.multiple_of(p * rows, 16), rows)
+        return pltpu.make_async_copy(turned.at[p % 2, k], turned_out.at[k, at, :], turn_sem.at[p % 2, k])
 
     def heads(p):
+        at = pl.ds(pl.multiple_of(p * rows, 16), rows)
+
+        @pl.when(p >= 2)
+        def _():
+            for k in range(4):
+                keep(p - 2, k).wait()
+
+        weights = []
+        for k in range(4):
+            part = slice(k * slab, (k + 1) * slab)
+            weights.append(jnp.concatenate([shards[i, at, :][:, part] for i in range(4)], axis=1))
+            turned[p % 2, k] = weights[k]
+            keep(p, k).start()
         known = normed[...]
-        at = pl.ds(pl.multiple_of(p * rows, 16), rows)
-        query = (nt(known, weights[0, at, :]) + t_query[p]).astype(jnp.bfloat16)
-        key = nt(known, weights[1, at, :]).astype(jnp.bfloat16)
-        value = (nt(known, weights[2, at, :]) + t_value[p]).astype(jnp.bfloat16)
+        hot = hots[...]
+        term = terms[4 * p] + terms[4 * p + 1] + terms[4 * p + 2] + terms[4 * p + 3]
+        query = (nt(known, weights[0]) + term[:, :rows]).astype(jnp.bfloat16)
+        key = nt(known, weights[1]).astype(jnp.bfloat16)
+        value = (nt(known, weights[2]) + term[:, rows : 2 * rows]).astype(jnp.bfloat16)
         queries[p] = query
         keys[p] = key
         values[p] = value
         outs = []
         for t in range(2):
             part = slice(t * size, (t + 1) * size)
-            scores = (nt(query[:, part], key[:, part]) + nt(places[2 * p + t], hots[...])) * scale
+            place_terms = sum(nn(hot, squares[k, 2 * p + t]) for k in range(3))
+            high = place_terms.astype(jnp.bfloat16)
+            rest = (place_terms - high.astype(jnp.float32)).astype(jnp.bfloat16)
+            scores = nt(query[:, part], key[:, part]) * scale + (nt(high, hot) + nt(rest, hot))
             scores = jnp.where(mask[...] > 0.0, scores, -1000000000.0)
             expo = jnp.exp(scores - jnp.max(scores, axis=-1, keepdims=True))
             low = (expo / jnp.sum(expo, axis=-1, keepdims=True)).astype(jnp.bfloat16)
@@ -318,50 +299,92 @@
             outs.append(nn(low, value[:, part]))
         attended[p] = jnp.concatenate(outs, axis=1).astype(jnp.bfloat16)
 
-    def work(step):
-        gather.step(step)
-
-        @pl.when(step == 0)
+    small.start(own_sem.at[0])
+
+    def first(step):
+        small.step(step)
+
+        @pl.when(step == 3)
         def _():
-            for copy in loads:
-                copy.wait()
-
-        heads(step)
-
-    every(SPOTS, work)
-    gather.finish()
-
-
-def attention_forward(block, small, normed, t_query, t_value, places, hots, mask, scale):
-    rows, width = block.shape[0] // 2, block.shape[1]
-    early = rows * 8 // 9
-    slots = normed.shape[0]
+            project()
+
+    every(SPOTS, first)
+    large.start(own_sem.at[1])
+    small.crossed(SPOTS - 1)
+    large.step(0)
+    small.all_here()
+    small.kept(own_sem.at[0])
+    every(31, lambda k: arrive(terms.at[(here + 31 - k) % 32], term_recv.at[k]))
+    large.step(1)
+
+    def second(n):
+        step = n + 2
+        large.step(step)
+
+        @pl.when(step < 4)
+        def _():
+            heads(2 * n)
+
+        heads(jnp.where(step < 4, 2 * n + 1, step))
+
+    every(SPOTS - 2, second)
+    large.crossed(SPOTS - 1)
+    for p in (SPOTS - 2, SPOTS - 1):
+        for k in range(4):
+            keep(p, k).wait()
+    large.all_here()
+    large.kept(own_sem.at[1])
+
+    def sent(k):
+        time_copy(k).wait_send()
+        term_copy(k).wait_send()
+
+    every(31, sent)
+    small.drain()
+    large.drain()
+
+
+def gathered_forward(small_block, block, times, w_times, normed, squares, hots, mask, scale):
+    rows, width = small_block.shape
+    slots, lanes = normed.shape[0], times.shape[2]
     dma = pltpu.SemaphoreType.DMA
     vmem, far = pl.BlockSpec(memory_space=pltpu.VMEM), pl.BlockSpec(memory_space=pl.ANY)
     low = block.dtype
     pair = jax.ShapeDtypeStruct((SPOTS, slots, rows), low)
+    terms = (32, 1, w_times.shape[1])
     return pl.pallas_call(
-        partial(attention_kernel, early, scale),
+        partial(forward_kernel, rows * 4 // 9, rows * 8 // 9, scale),
         out_shape=(
             jax.ShapeDtypeStruct((SPOTS * rows, 4 * width), low),
             jax.ShapeDtypeStruct((32 * rows, width), low),
+            jax.ShapeDtypeStruct((4, SPOTS * rows, width), low),
+            jax.ShapeDtypeStruct((32, lanes), jnp.float32),
             pair,
             pair,
             pair,
             jax.ShapeDtypeStruct((2 * SPOTS, slots, slots), low),
             pair,
         ),
-        in_specs=[vmem, far] + [vmem] * 6,
-        out_specs=(far, far) + (vmem,) * 5,
+        in_specs=[vmem] * 8,
+        out_specs=(far,) * 3 + (vmem,) * 6,
         scratch_shapes=[
-            pltpu.VMEM((3, SPOTS * rows, width), low),
-            dma((3,)),
-            dma((3,)),
+            pltpu.VMEM((4, SPOTS * rows, width), low),
+            pltpu.VMEM((2, 4, rows, width), low),
+            pltpu.VMEM((32, 1, lanes), jnp.float32),
+            pltpu.VMEM(terms, jnp.float32),
+            pltpu.VMEM(terms, jnp.float32),
+            dma((2, 3)),
+            dma((2, 4)),
+            dma((31,)),
+            dma((31,)),
+            dma((31,)),
+            dma((31,)),
+            *Gather.semaphores(2, 1),
             *Gather.semaphores(3, 1),
         ],
-        compiler_params=pltpu.CompilerParams(collective_id=1, has_side_effects=True, vmem_limit_bytes=60 << 20),
+        compiler_params=pltpu.CompilerParams(collective_id=0, has_side_effects=True, vmem_limit_bytes=60 << 20),
         name="attention_forward",
-    )(block, small, normed, t_query, t_value, places, hots, mask)
+    )(small_block, block, times, w_times, normed, squares, hots, mask)
 
 
 def pile(target, sources, size):
@@ -556,12 +579,13 @@
 
 
 def backward_kernel(
-    early, scale, down_in, up_in, small_in, normed, grad_attended, queries, keys, values, probs, hots, result, small_out,
+    early, scale, down_in, up_in, small_in, normed, attended, grad_mixed, grad_attended, queries, keys, values, probs, hots,
+    result, small_out,
     grad_normed, squares, sums, weights, load_sem, grads, grad_sem, *scratch,
 ):
     rows, width = result.shape[0] // 2, result.shape[1]
     size = rows // 2
-    sides = hots.shape[1]
+    slab = width // 4
     greet()
     loads = [pltpu.make_async_copy(small_in.at[k], weights.at[k], load_sem.at[k]) for k in range(3)]
     for copy in loads:
@@ -603,20 +627,25 @@
 
         @pl.when(p >= 2)
         def _():
-            for k in range(3):
+            for k in range(4):
                 keep(p - 2, k).wait()
 
         known = normed[...]
         at = pl.ds(pl.multiple_of(p * rows, 16), rows)
         total = None
+        turned = []
         for k in range(3):
             grad = jnp.concatenate(parts[k], axis=1).astype(jnp.bfloat16)
             sums[k, p] = jnp.sum(grad.astype(jnp.float32), axis=0, keepdims=True)
-            grads[p % 2, k] = tn(grad, known).astype(jnp.bfloat16)
-            keep(p, k).start()
+            turned.append(tn(grad, known).astype(jnp.bfloat16))
             term = nn(grad, weights[k, at, :])
             total = term if total is None else total + term
         grad_normed[...] += total
+        turned.append(tn(grad_mixed[p], attended[...]).astype(jnp.bfloat16))
+        for k in range(4):
+            part = slice(k * slab, (k + 1) * slab)
+            grads[p % 2, k] = jnp.concatenate([rows_of[:, part] for rows_of in turned], axis=1)
+            keep(p, k).start()
 
     def work(step):
         @pl.when(step < SPOTS - 1)
@@ -632,12 +661,14 @@
 
     every(SPOTS, work)
     for p in (SPOTS - 2, SPOTS - 1):
-        for k in range(3):
+        for k in range(4):
             keep(p, k).wait()
     scatter.finish()
 
 
-def attention_backward(down, up, small, normed, grad_attended, queries, keys, values, probs, hots, scale):
+def attention_backward(
+    down, up, small, normed, attended, grad_mixed, grad_attended, queries, keys, values, probs, hots, scale
+):
     rows, width = up.shape[0] // 32, up.shape[1]
     early = rows * 8 // 9
     slots = normed.shape[0]
@@ -649,23 +680,23 @@
         partial(backward_kernel, early, scale),
         out_shape=(
             jax.ShapeDtypeStruct((2 * rows, width), jnp.float32),
-            jax.ShapeDtypeStruct((3, SPOTS * rows, width), low),
+            jax.ShapeDtypeStruct((4, SPOTS * rows, width), low),
             jax.ShapeDtypeStruct((slots, width), jnp.float32),
             jax.ShapeDtypeStruct((2 * SPOTS, sides, sides), jnp.float32),
             jax.ShapeDtypeStruct((3, SPOTS, 1, rows), jnp.float32),
         ),
-        in_specs=[far] * 3 + [vmem] * 7,
+        in_specs=[far] * 3 + [vmem] * 9,
         out_specs=(vmem, far, vmem, vmem, vmem),
         scratch_shapes=[
             pltpu.VMEM((3, SPOTS * rows, width), low),
             dma((3,)),
-            pltpu.VMEM((2, 3, rows, width), low),
-            dma((2, 3)),
+            pltpu.VMEM((2, 4, rows, width), low),
+            dma((2, 4)),
             *Scatter.scratch(2, rows, early, width, low),
         ],
         compiler_params=pltpu.CompilerParams(collective_id=2, has_side_effects=True, vmem_limit_bytes=63 << 20),
         name="attention_backward",
-    )(down, up, small, normed, grad_attended, queries, keys, values, probs, hots)
+    )(down, up, small, normed, attended, grad_mixed, grad_attended, queries, keys, values, probs, hots)
 
 
 def last_sums_kernel(early, small_in, out_in, extra_in, result, extra_out, own_sem, note_sems, scratch):
@@ -681,8 +712,8 @@
 
     scatter = Scatter(home, 1, rows, early, result, *scratch)
     scatter.begin()
-    notes = Gather(note, 1, 1, *note_sems)
-    keep_own([(extra_in, note(0, owner(x, core, spot)))], own_sem)
+    notes = Gather(lambda k: extra_in, note, 1, 1, *note_sems)
+    notes.start(own_sem)
 
     def work(step):
         notes.step(step)
@@ -693,7 +724,9 @@
 
     every(SPOTS, work)
     scatter.finish()
-    notes.finish()
+    notes.all_here()
+    notes.kept(own_sem)
+    notes.drain()
 
 
 def last_sums(small, extra):
@@ -893,42 +926,34 @@
     def outer(grads, values):
         return jnp.einsum("re,rd->ed", grads, values, preferred_element_type=jnp.float32).astype(jnp.bfloat16)
 
-    small = jnp.stack([w_query.T, w_key.T, w_value.T, w_out.T])
-    wide = w_up.T.reshape(4, rows, slab)
-    swapped = lax.all_to_all(jnp.stack([small, wide], axis=1), "inner", 0, 0)
-    joined = jnp.transpose(swapped, (1, 2, 0, 3)).reshape(2, rows, width)
+    small = jnp.concatenate([w_query.T, w_key.T, w_value.T, w_out.T], axis=1)
+    swapped = lax.all_to_all(w_up.T.reshape(4, rows, slab), "inner", 0, 0)
+    wide = jnp.transpose(swapped, (1, 0, 2)).reshape(rows, width)
     w_times = jnp.concatenate([w_time_query, w_time_value], axis=1)
     w_times = jnp.pad(w_times, ((0, -slab % 128), (0, -2 * rows % 128)))
     times = time_vec.astype(jnp.float32).reshape(4, 1, slab)
     times = jnp.pad(times, ((0, 0), (0, 0), (0, -slab % 128)))
-    t_small, all_times, terms = attention_gather(joined[0], times, w_times)
-    all_times = all_times[:, :slab]
-    terms = terms.reshape(SPOTS, 4, -1)[:, :, : 2 * rows].sum(axis=1).reshape(SPOTS, 1, 2 * rows)
-
     inputs = tokens.astype(jnp.float32).reshape(slots, width)
     normed_attn = layer_norm(inputs, gain_attn).astype(jnp.bfloat16)
     usable, row_place, col_place = slot_positions(grid, slots)
     offset_hot = offset_table()
     hot = jnp.concatenate([side_hot(row_place)[0], side_hot(col_place)[0]], axis=1)
-    squares = [
+    square = [
         jnp.einsum("hd,rsd->hrs", table, offset_hot, precision=PRECISE) for table in (bias_rows, bias_cols)
     ]
-    places = jnp.concatenate(
-        [
-            jnp.einsum("ir,hrs->his", hot[:, GS * k : GS * (k + 1)], squares[k] / scale, precision=PRECISE)
-            for k in range(2)
-        ],
-        axis=2,
+    square = jnp.concatenate(
+        [jnp.pad(square[0], ((0, 0), (0, 0), (0, GS))), jnp.pad(square[1], ((0, 0), (0, 0), (GS, 0)))], axis=1
     )
-    high = lax.reduce_precision(places, 8, 7)
-    places = jnp.concatenate([high, places - high], axis=2).astype(jnp.bfloat16)
+    first = lax.reduce_precision(square, 8, 7)
+    second = lax.reduce_precision(square - first, 8, 7)
+    squares = jnp.stack([first, second, square - first - second]).astype(jnp.bfloat16)
     hot = hot.astype(jnp.bfloat16)
-    hots = jnp.concatenate([hot, hot], axis=1)
     mask = usable.astype(jnp.float32)
-    block = jnp.concatenate([w_down.T, joined[1]], axis=0)
-    t_down, t_up, queries, keys, values, probs, attended = attention_forward(
-        block, t_small, normed_attn, terms[:, :, :rows], terms[:, :, rows:], places, hots, mask, scale
+    block = jnp.concatenate([w_down.T, wide], axis=0)
+    t_down, t_up, t_small, all_times, queries, keys, values, probs, attended = gathered_forward(
+        small, block, times, w_times, normed_attn, squares, hot, mask, scale
     )
+    all_times = all_times[:, :slab]
     attended = jnp.transpose(attended, (1, 0, 2)).reshape(slots, width)
     mixed = inputs + ahead(attended, t_small[3])
     normed_mlp = layer_norm(mixed, gain_mlp).astype(jnp.bfloat16)
@@ -949,12 +974,15 @@
     grad_mixed_norm, grad_gain_mlp = norm_mlp_back(grad_normed_mlp)
     grad_mixed = upstream + grad_mixed_norm
     grad_mixed_low = grad_mixed.astype(jnp.bfloat16)
-    grad_out = outer(grad_mixed_low, attended)
     grad_attended = back(grad_mixed_low, t_small[3]).astype(jnp.bfloat16)
     grad_attended = jnp.transpose(grad_attended.reshape(slots, SPOTS, rows), (1, 0, 2))
+    mixed_pairs = jnp.transpose(grad_mixed_low.reshape(slots, SPOTS, rows), (1, 0, 2))
     wide_block, small_grads, grad_normed_attn, table_squares, slot_sums = attention_backward(
-        grad_down, grad_up, t_small, normed_attn, grad_attended, queries, keys, values, probs, hot, scale
+        grad_down, grad_up, t_small, normed_attn, attended, mixed_pairs, grad_attended, queries, keys, values, probs, hot,
+        scale,
     )
+    parted = jnp.transpose(wide_block[rows:].astype(jnp.bfloat16).reshape(rows, 4, slab), (1, 0, 2))
+    swapped = lax.all_to_all(parted, "inner", 0, 0).astype(jnp.float32)
     unused_attn, norm_attn_back = jax.vjp(layer_norm, inputs, gain_attn)
     grad_inputs_norm, grad_gain_attn = norm_attn_back(grad_normed_attn)
     grad_tokens = (grad_mixed + grad_inputs_norm).astype(jnp.bfloat16).reshape(images, slots, width)
@@ -965,15 +993,12 @@
     own = (grad_gain_attn, grad_gain_mlp, *tables, slot_sums[0], slot_sums[2])
     notes = jnp.stack([jnp.pad(value.reshape(-1), (0, width - value.size)) for value in own])
     notes = jnp.pad(notes, ((0, 2), (0, 0)))
-    small_block, notes = last_sums(jnp.concatenate([small_grads, grad_out[None]], axis=0), notes)
+    small_block, notes = last_sums(small_grads, notes)
     totals = notes[:, :4].sum(axis=0)
     entries = bias_rows.size
     table = bias_rows.shape
-    joined = jnp.stack([small_block, wide_block[rows:]]).astype(jnp.bfloat16)
-    parted = jnp.transpose(joined.reshape(2, rows, 4, slab), (2, 0, 1, 3))
-    swapped = lax.all_to_all(parted, "inner", 0, 0).astype(jnp.float32)
-    grad_small = jnp.transpose(swapped[:, 0], (0, 2, 1))
-    grad_up = swapped[:, 1].reshape(4 * rows, slab).T
+    grad_small = [small_block[:, slab * k : slab * (k + 1)].T for k in range(4)]
+    grad_up = swapped.reshape(4 * rows, slab).T
     grad_down = wide_block[:rows].T
     return (
         output,

time: 478 us -> 455 us (0.952)
  other arithmetic: 33.3 us -> 14.6 us
  local copies, waits for them, and re-layouts: 22.2 us -> 28.6 us
  waiting for transfers between devices: 7.97 us -> 3.04 us
    concatenate x4 -> x1, other arithmetic: 13.4 us -> 0.89 us  [by_rings(): block = jnp.concatenate([w_down.T, wide], axis=0)]
    pallas_call x2 -> x1, Pallas kernels: 150 us -> 138 us  [gathered_forward(): pl.pallas_call(partial(forward_kernel, rows * 4 // 9, rows * 8 // 9, scal...]
    pallas_call x1, Pallas kernels: 111 us -> 118 us  [attention_backward(): pl.pallas_call(partial(backward_kernel, early, scale), out_shape=(jax.Sha...]
    dot_general x2 -> x0, matrix products: 5.49 us -> none  [by_rings(): jnp.einsum('ir,hrs->his', hot[:, GS * k:GS * (k + 1)], squares[k] / scale...]
    all_to_all x1, waiting for transfers between devices: 7.97 us -> 3.03 us  [by_rings(): swapped = lax.all_to_all(parted, 'inner', 0, 0).astype(jnp.float32)]
    dot_general x3 -> x2, matrix products: 21.4 us -> 19.7 us  [outer(): jnp.einsum('re,rd->ed', grads, values, preferred_element_type=jnp.float32)]
  transfers between devices with their start and end apart: 2 -> 2, of which waited for: 1 -> 1; matrix products, arithmetic and copies ran while one was open for 5% -> 4% of each run, Pallas kernels for 0% -> 0%
where the time goes in v1:
time: 455 us; the launch traced here: 447 us
  Pallas kernels  318 us (70%)
  matrix products  69.7 us (15%)
  local copies, waits for them, and re-layouts  28.6 us (6%)
  other arithmetic  14.6 us (3%)
  starting transfers between devices  7.83 us (2%)
  between operations  4.86 us (1%)
    pallas_call x1, Pallas kernels, gathered_forward(): pl.pallas_call(partial(forward_kernel, rows * 4 // 9, rows * 8 // 9, scal...  138 us
    pallas_call x1, Pallas kernels, attention_backward(): pl.pallas_call(partial(backward_kernel, early, scale), out_shape=(jax.Sha...  118 us
    pallas_call x1, Pallas kernels, last_sums(): pl.pallas_call(kernel, out_shape=(jax.ShapeDtypeStruct((rows, width), jnp...  61.5 us
    dot_general x2, matrix products, outer(): jnp.einsum('re,rd->ed', grads, values, preferred_element_type=jnp.float32)  19.7 us
    dot_general x1, matrix products, by_rings(): result = jnp.where(keep_rows, mixed + ahead(hidden, t_down), 0.0)  11.5 us
    dot_general x1, matrix products, by_rings(): grad_hidden = back(upstream_low, t_down)  9.51 us
    dot_general x1, matrix products, by_rings(): grad_normed_mlp = back(grad_up_proj, t_up)  9.22 us
  transfers between devices with their start and end apart: 2, of which 1 were waited for; matrix products, arithmetic and copies ran while one was open for 4% of the time, Pallas kernels for 0%

profile of v1, /device:TPU:0, one launch (start us, length us, event | category | flops | bytes accessed | tf_op | source)
XLA Modules:
  0.0 446.5 jit_solution(15388397052378443782)
XLA Ops:
  0.7 2.0 copy.39
  2.7 4.4 all-to-all-start
  23.2 138.2 %attention_forward.1 = (bf16[1152,4608]{1,0:T(8,128)(2,1)}, bf16[4608,1152]{1,0:T(8,128)(2,1)}, bf16[4,1152,1152]{2,1,0:T(8,128)(2,1)}, f32[32,384]{1,0:T(8,128)...) custom-call(bf16[144,1152]{1,0:T(8,128)(2,1)} %concatenate.46.small_, ...), custom_call_target="tpu_custom_call" | custom-call | tf_op jit(solution)/shard_map/attention_forward/pallas_call | solution.py:355
  161.4 1.8 copy.46
  163.1 1.4 copy.51.attended
  164.6 3.3 fusion.75
  168.5 7.0 %fusion.70 = f32[320,4608]{1,0:T(8,128)S(1)} fusion(bf16[4608,1152]{1,0:T(8,128)(2,1)} %get-tuple-element.32, f32[320,1152]{1,0:T(8,128)S(1)} %get-tuple-element.86, f32[1152]{0:T(1024)S(1)} %copy-done.24, f32[320]{0:T(512)S(1)} %fusion.62, f32[320]{0:T(512)S(1)} %broadcast_multiply_fusion), kind=kOutput, calls=%fused_computation.136 | convolution fusion | flops 3398860800 | bytes 17996800 | tf_op jit(solution)/shard_map/rd,ed->re/dot_general | solution.py:960
  175.6 11.5 %fusion.11 = bf16[1,320,1152]{2,1,0:T(8,128)(2,1)} fusion(f32[320,1152]{1,0:T(8,128)S(1)} %get-tuple-element.86, bf16[1152,4608]{1,0:T(8,128)(2,1)} %get-tuple-element.33, pred[320]{0:T(512)(128)(4,1)S(1)} %iota_compare_fusion.9, f32[320,4608]{1,0:T(8,128)S(1)} %fusion.70), kind=kOutput, calls=%fused_computation.19 | convolution fusion | flops 3411763200 | bytes 18727232 | tf_op jit(solution)/shard_map/rd,ed->re/dot_general | solution.py:963
  187.1 9.5 %fusion.6 = bf16[320,4608]{1,0:T(8,128)(2,1)S(1)} fusion(f32[320,4608]{1,0:T(8,128)S(1)} %fusion.70, bf16[1152,4608]{1,0:T(8,128)(2,1)} %get-tuple-element.33, bf16[1,320,1152]{2,1,0:T(8,128)(2,1)S(1)} %copy-done.6, pred[320]{0:T(512)(128)(4,1)S(1)} %iota_compare_fusion.9), kind=kOutput, calls=%fused_computation.10 | convolution fusion | flops 3427983360 | bytes 20201792 | tf_op jit(solution)/shard_map/re,ed->rd/dot_general | solution.py:968
  196.7 9.2 %multiply_reduce_fusion = (f32[1152]{0:T(1024)S(1)}, f32[320]{0:T(512)S(1)}, f32[320,1152]{1,0:T(8,128)S(1)}) fusion(f32[320,1152]{1,0:T(8,128)S(1)} %get-tuple-element.86, f32[320]{0:T(512)S(1)} %fusion.62, f32[320]{0:T(512)S(1)} %broadcast_multiply_fusion, f32[1152]{0:T(1024)S(1)} %copy-done.24, bf16[320,4608]{1,0:T(8,128)(2,1)S(1)} %fusion.6, ...), kind=kOutput, calls=%fused_computation.40 | convolution fusion | flops 3399965440 | bytes 16528128 | tf_op jit(solution)/shard_map/re,ed->rd/dot_general | solution.py:972
  208.5 3.9 convolution_convert_fusion.2
  212.4 2.2 copy.47
  214.6 10.7 %convolution_convert_fusion.1.down_in = bf16[1152,4608]{1,0:T(8,128)(2,1)} fusion(bf16[1,320,1152]{2,1,0:T(8,128)(2,1)S(1)} %copy-done.6, pred[320]{0:T(512)(128)(4,1)S(1)} %iota_compare_fusion.9, f32[320,4608]{1,0:T(8,128)} %copy-done.8), kind=kOutput, calls=%fused_computation.1 | convolution fusion | flops 3417071616 | bytes 17252672 | tf_op jit(solution)/shard_map/re,rd->ed/dot_general | solution.py:927
  225.3 9.0 %convolution_convert_fusion.up_in = bf16[4608,1152]{1,0:T(8,128)(2,1)} fusion(bf16[320,4608]{1,0:T(8,128)(2,1)S(1)} %copy-done.29, f32[320,1152]{1,0:T(8,128)S(1)} %get-tuple-element.86, f32[1152]{0:T(1024)S(1)} %copy-done.24, f32[320]{0:T(512)S(1)} %fusion.62, f32[320]{0:T(512)S(1)} %broadcast_multiply_fusion), kind=kOutput, calls=%fused_computation | convolution fusion | flops 3404169216 | bytes 15047680 | tf_op jit(solution)/shard_map/re,rd->ed/dot_general | solution.py:927
  235.1 1.8 copy.50
  236.9 1.5 copy.48
  238.5 118.3 %attention_backward.1 = (f32[288,1152]{1,0:T(8,128)}, bf16[4,1152,1152]{2,1,0:T(8,128)(2,1)}, f32[320,1152]{1,0:T(8,128)}, f32[16,64,64]{2,1,0:T(8,128)}, f32[3,8,1,144]{3,2,1,0:T(1,128)}) custom-call(bf16[1152,4608]{1,0:T(8,128)(2,1)} %convolution_convert_fusion.1.down_in, bf16[4608,1152]{1,0:T(8,128)(2,1)} %convolution_convert_fusion.up_in, ...), custom_call_target="tpu_custom_call" | custom-call | tf_op jit(solution)/shard_map/attention_backward/pallas_call | solution.py:679
  358.0 2.0 slice_bitcast_fusion
  363.6 61.5 %last_sums.1 = (f32[144,1152]{1,0:T(8,128)}, f32[32,8,1152]{2,1,0:T(8,128)}) custom-call(bf16[4,1152,1152]{2,1,0:T(8,128)(2,1)} %get-tuple-element.39.small_in, f32[8,1152]{1,0:T(8,128)} %pad.36.extra_in), custom_call_target="tpu_custom_call" | custom-call | tf_op jit(solution)/shard_map/last_sums/pallas_call | solution.py:741
  425.2 1.4 slice_reduce_fusion
  426.6 1.9 fusion.72
  429.2 3.0 fusion.28
  433.4 3.5 all-to-all-start.1
  441.7 3.0 all-to-all-done.1
  (132 shorter events, 29.6 us)
Async XLA Ops:
  0.6 13.4 %copy-start = (f32[16,63]{1,0:T(8,128)S(1)}, f32[16,63]{1,0:T(8,128)}, u32[]{:S(2)}) copy-start(f32[16,63]{1,0:T(8,128)} %param.30) | copy-start | bytes 12100
  0.7 6.4 %copy-start.26 = (s32[1,2]{1,0:T(1,128)S(1)}, s32[1,2]{1,0:T(1,128)}, u32[]{:S(2)}) copy-start(s32[1,2]{1,0:T(1,128)} %param.18) | copy-start | bytes 28
  0.7 10.8 %copy-start.2 = (bf16[1,320,1152]{2,1,0:T(8,128)(2,1)S(1)}, bf16[1,320,1152]{2,1,0:T(8,128)(2,1)}, u32[]{:S(2)}) copy-start(bf16[1,320,1152]{2,1,0:T(8,128)(2,1)} %param.16) | copy-start | bytes 2211844
  0.7 11.4 %copy-start.25 = (bf16[1,1152]{1,0:T(2,128)(2,1)S(1)}, bf16[1,1152]{1,0:T(2,128)(2,1)}, u32[]{:S(2)}) copy-start(bf16[1,1152]{1,0:T(2,128)(2,1)} %param.17) | copy-start | bytes 6916
  0.7 13.1 %copy-start.21 = (bf16[288,144]{0,1:T(8,128)(2,1)S(1)}, bf16[288,144]{0,1:T(8,128)(2,1)}, u32[]{:S(2)}) copy-start(bf16[288,144]{0,1:T(8,128)(2,1)} %param.25) | copy-start | bytes 248836
  2.7 11.2 %copy-start.22 = (bf16[288,144]{0,1:T(8,128)(2,1)S(1)}, bf16[288,144]{0,1:T(8,128)(2,1)}, u32[]{:S(2)}) copy-start(bf16[288,144]{0,1:T(8,128)(2,1)} %param.26) | copy-start | bytes 248836
  2.7 19.1 %all-to-all-start = ((bf16[4,144,288]{2,1,0:T(8,128)(2,1)}), bf16[4,144,288]{2,1,0:T(8,128)(2,1)S(1)}, u32[]{:S(2)}, u32[]{:S(2)}) async-start(bf16[4,144,288]{2,1,0:T(8,128)(2,1)} %bitcast.8), calls=%async_computation | async-start | bytes 884736 | tf_op jit(solution)/shard_map/all_to_all | solution.py:930
  11.5 3.8 copy-start.27
  17.5 1.4 copy-start.17
  17.5 1.4 copy-start.18
  20.7 1.6 copy-start.14
  175.6 11.6 %copy-start.8 = (f32[320,4608]{1,0:T(8,128)}, f32[320,4608]{1,0:T(8,128)S(1)}, u32[]{:S(2)}) copy-start(f32[320,4608]{1,0:T(8,128)S(1)} %fusion.70) | copy-start | bytes 17694724
  175.6 11.5 %copy-start.6 = (bf16[1,320,1152]{2,1,0:T(8,128)(2,1)S(1)}, bf16[1,320,1152]{2,1,0:T(8,128)(2,1)}, u32[]{:S(2)}) copy-start(bf16[1,320,1152]{2,1,0:T(8,128)(2,1)} %param.19) | copy-start | bytes 2211844
  196.7 9.2 %copy-start.28 = (bf16[320,4608]{1,0:T(8,128)(2,1)}, bf16[320,4608]{1,0:T(8,128)(2,1)S(1)}, u32[]{:S(2)}) copy-start(bf16[320,4608]{1,0:T(8,128)(2,1)S(1)} %fusion.6) | copy-start | bytes 8847364
  214.6 10.7 %copy-start.29 = (bf16[320,4608]{1,0:T(8,128)(2,1)S(1)}, bf16[320,4608]{1,0:T(8,128)(2,1)}, u32[]{:S(2)}) copy-start(bf16[320,4608]{1,0:T(8,128)(2,1)} %copy-done.28) | copy-start | bytes 8847364
  225.3 9.0 %copy-start.12 = (bf16[320,1152]{1,0:T(8,128)(2,1)S(1)}, bf16[320,1152]{1,0:T(8,128)(2,1)}, u32[]{:S(2)}) copy-start(bf16[320,1152]{1,0:T(8,128)(2,1)} %convolution_convert_fusion.2) | copy-start | bytes 2211844
  235.1 1.8 copy-start.9
  356.7 3.2 copy-start.5
  363.6 65.5 %copy-start.4 = (f32[320,1152]{1,0:T(8,128)S(1)}, f32[320,1152]{1,0:T(8,128)}, u32[]{:S(2)}) copy-start(f32[320,1152]{1,0:T(8,128)} %copy-done.3) | copy-start | bytes 4423684
  425.1 4.0 copy-start.7
  432.2 6.4 %copy-start.15 = (f32[32,384]{1,0:T(8,128)S(1)}, f32[32,384]{1,0:T(8,128)}, u32[]{:S(2)}) copy-start(f32[32,384]{1,0:T(8,128)} %get-tuple-element.44) | copy-start | bytes 147460
  432.2 8.5 %copy-start.11 = (f32[144,1152]{1,0:T(8,128)S(1)}, f32[144,1152]{1,0:T(8,128)}, u32[]{:S(2)}) copy-start(f32[144,1152]{1,0:T(8,128)} %get-tuple-element.43) | copy-start | bytes 1990660
  433.4 11.4 %all-to-all-start.1 = ((bf16[4,144,288]{2,1,0:T(8,128)(2,1)}), bf16[4,144,288]{2,1,0:T(8,128)(2,1)S(1)}, u32[]{:S(2)}, u32[]{:S(2)}) async-start(bf16[4,144,288]{2,1,0:T(8,128)(2,1)} %bitcast.122), calls=%async_computation.1 | async-start | bytes 884736 | tf_op jit(solution)/shard_map/all_to_all | solution.py:985
  440.7 5.4 %copy-start.1 = (f32[16,63]{1,0:T(8,128)S(1)}, f32[16,63]{1,0:T(8,128)}, u32[]{:S(2)}) copy-start(f32[16,63]{1,0:T(8,128)} %param.30) | copy-start | bytes 12100
  (8 other events, 8.6 us)
